TPU v7x, 8 devices: a whole 2x2x1 slice. The times are simulated.
8 devices in a mesh: dp: 8 (over z, y, x, core).
Axes of the slice: x: 2, y: 2, z: 1, core: 2. Of those that a mesh axis runs over, the one named last changes fastest.
Arguments:
- img_emb: bfloat16 [32768, 512], P('dp')
- txt_emb: bfloat16 [32768, 512], P('dp')
- log_temp: float32 [1], replicated
- logit_bias: float32 [1], replicated
Outputs:
- output 1: float32 [1], replicated
- output 2: float32 [32768, 512], P('dp')
- output 3: float32 [32768, 512], P('dp')
- output 4: float32 [1], replicated
- output 5: float32 [1], replicated
All inputs are finite; a program needn't handle non-finite values.
Results may differ from a plain program's by a relative error of at most 0.001.
Values are sent between devices in bfloat16 or wider.
A program may use at most 1 GiB of HBM per device.

v0:
```python
import functools
import jax
import jax.numpy as jnp
from jax import lax
from jax.experimental import pallas as pl
from jax.experimental.pallas import tpu as pltpu
from jax.sharding import PartitionSpec as P


F32 = jnp.float32
BF16 = jnp.bfloat16
CLAMP = 31.0
LOG2E = 1.4426950408889634
LN2 = 0.6931471805599453
TILE = 1024
PIECE_M = 256
PIECE_N = 512
NN = (((1,), (0,)), ((), ()))
NT = (((1,), (1,)), ((), ()))
TN = (((0,), (0,)), ((), ()))


def dot(a, b, dims):
    return lax.dot_general(a, b, dims, preferred_element_type=F32)


def fold(x):
    m, n = x.shape
    x = jnp.sum(x.reshape(m // 8, 8, n), axis=0)
    return sum(x[:, k * 128:(k + 1) * 128] for k in range(n // 128))


def pair_terms(y, flip):
    if flip is not None:
        y = jnp.where(flip, -y, y)
    e = jnp.exp2(jnp.minimum(y, CLAMP))
    d = 1.0 + e
    c = e * (1.0 / d)
    h = e.shape[0] // 4
    e0, e1, e2, e3 = (e[k * h:(k + 1) * h] for k in range(4))
    qa = e0 * d[h:2 * h] + e1
    qb = e2 * d[3 * h:] + e3
    q = qa * (1.0 + qb) + qb
    dq = 1.0 + q
    log_part = jnp.log2(dq)
    rest_part = (q - (dq - 1.0)) * (1.0 / dq)
    if flip is not None:
        c = jnp.where(flip, -c, c)
    return c, log_part, rest_part


def block_kernel(*refs, diag, img_outer, i0, j0, keep_init, extra, fresh_from):
    it = iter(refs)
    sc_ref, img_ref, txt_ref = next(it), next(it), next(it)
    stream_in = next(it)
    keep_in = next(it) if keep_init else None
    keep_extra = next(it) if extra else None
    st_in, stream_ref, keep_ref, st_ref, coef = it
    outer, inner = pl.program_id(0), pl.program_id(1)
    i, j = (outer, inner) if img_outer else (inner, outer)
    s2 = sc_ref[0]
    b2 = sc_ref[1]

    @pl.when((outer == 0) & (inner == 0))
    def _():
        st_ref[...] = st_in[...]

    @pl.when(inner == 0)
    def _():
        base = keep_in[...] if keep_init else jnp.zeros_like(keep_ref)
        keep_ref[...] = base + keep_extra[...] if extra else base

    if fresh_from is not None:
        @pl.when((outer == 0) & (inner >= fresh_from))
        def _():
            stream_in[...] = jnp.zeros_like(stream_in)

    if img_outer:
        ig_ref, tg_ref, ig_base, tg_base = keep_ref, stream_ref, keep_ref, stream_in
    else:
        ig_ref, tg_ref, ig_base, tg_base = stream_ref, keep_ref, stream_in, keep_ref

    def flip_mask(m, n, rows, cols):
        row = lax.broadcasted_iota(jnp.int32, (rows, cols), 0) + ((i0 + i) * TILE + m)
        col = lax.broadcasted_iota(jnp.int32, (rows, cols), 1) + ((j0 + j) * TILE + n)
        return row == col

    for n in range(0, TILE, PIECE_N):
        for m in range(0, TILE, PIECE_M):
            dots = dot(img_ref[m:m + PIECE_M, :], txt_ref[n:n + PIECE_N, :], NT)
            flip = flip_mask(m, n, PIECE_M, PIECE_N) if diag else None
            c, log_part, rest_part = pair_terms(dots * s2 + b2, flip)
            coef[m:m + PIECE_M, n:n + PIECE_N] = c.astype(BF16)
            st_ref[0] += fold(log_part)
            st_ref[1] += fold(rest_part)
            st_ref[2] += fold(c)
            st_ref[3] += fold(c * dots)
        tg_ref[n:n + PIECE_N, :] = tg_base[n:n + PIECE_N, :] + dot(coef[:, n:n + PIECE_N], img_ref[...], TN)
    ig_ref[...] = ig_base[...] + dot(coef[...], txt_ref[...], NN)

    @pl.when(sc_ref[2] > 0.0)
    def _():
        @pl.loop(0, TILE // 256)
        def _(k):
            m = pl.multiple_of(k * 256, 256)
            y = dot(img_ref[pl.ds(m, 256), :], txt_ref[...], NT) * s2 + b2
            if diag:
                y = jnp.where(flip_mask(m, 0, 256, TILE), 0.0, y)
            st_ref[0] += fold(jnp.maximum(y - CLAMP, 0.0))

    if diag:
        @pl.when((sc_ref[3] > 0.0) & (i0 + i == j0 + j))
        def _():
            own = jnp.sum(img_ref[...].astype(F32) * txt_ref[...].astype(F32), axis=1, keepdims=True)
            excess = jnp.maximum(-(own * s2 + b2) - CLAMP, 0.0)
            st_ref[0] += fold(jnp.broadcast_to(excess, (TILE, 128))) * (1.0 / 128.0)


def block_call(sc, img, txt, stream, keep, st, *, diag=False, img_outer=True, irange=None, jrange=None, keep_off=0, keep_rows=None, extra=None, fresh_from=None):
    dim = img.shape[1]
    i0, i1 = irange or (0, img.shape[0] // TILE)
    j0, j1 = jrange or (0, txt.shape[0] // TILE)
    ni, nj = i1 - i0, j1 - j0
    if img_outer:
        grid, o0, n0 = (ni, nj), i0, j0
    else:
        grid, o0, n0 = (nj, ni), j0, i0
    ospec = lambda off: pl.BlockSpec((TILE, dim), lambda a, b: (a + off, 0))
    nspec = lambda off: pl.BlockSpec((TILE, dim), lambda a, b: (b + off, 0))
    keep_rows = keep_rows or (img if img_outer else txt).shape[0]
    sspec = pl.BlockSpec(st.shape, lambda a, b: (0, 0, 0))
    in_specs = [pl.BlockSpec(memory_space=pltpu.SMEM)]
    in_specs += [ospec(i0), nspec(j0)] if img_outer else [nspec(i0), ospec(j0)]
    in_specs += [nspec(n0)]
    args = [sc, img, txt, stream]
    alias = {3: 0}
    out_off = o0 - keep_off
    if keep is not None:
        in_off = o0 if keep.shape[0] > keep_rows else out_off
        if keep.shape[0] == keep_rows:
            alias[len(args)] = 1
        args.append(keep)
        in_specs.append(ospec(in_off))
    if extra is not None:
        args.append(extra)
        in_specs.append(ospec(o0))
    alias[len(args)] = 2
    args.append(st)
    in_specs.append(sspec)
    pairs = ni * nj * TILE * TILE
    kernel = functools.partial(
        block_kernel, diag=diag, img_outer=img_outer, i0=i0, j0=j0, keep_init=keep is not None, extra=extra is not None, fresh_from=fresh_from
    )
    return pl.pallas_call(
        kernel,
        grid=grid,
        in_specs=in_specs,
        out_specs=[nspec(n0), ospec(out_off), sspec],
        out_shape=[
            jax.ShapeDtypeStruct(stream.shape, F32),
            jax.ShapeDtypeStruct((keep_rows, dim), F32),
            jax.ShapeDtypeStruct(st.shape, F32),
        ],
        scratch_shapes=[pltpu.VMEM((TILE, TILE), BF16)],
        input_output_aliases=alias,
        compiler_params=pltpu.CompilerParams(dimension_semantics=("arbitrary", "arbitrary"), vmem_limit_bytes=48 * 2**20),
        cost_estimate=pl.CostEstimate(flops=6 * pairs * dim, transcendentals=3 * pairs, bytes_accessed=40 * 2**20),
        name="pair_block",
    )(*args)


def solution(mesh):
    axis_name = mesh.axis_names[0]
    n_dev = mesh.shape[axis_name]

    def swap(x, bit):
        return lax.ppermute(x, axis_name, [(d, d ^ bit) for d in range(n_dev)])

    CORE, X, Y = 1, 2, 4

    def per_device(img_own, txt_own, log_temp, logit_bias):
        rows, dim = img_own.shape
        n_total = rows * n_dev
        nb = rows // TILE
        half = nb // 2
        cut = half * TILE
        scale = jnp.exp(log_temp[0])
        bias = logit_bias[0]
        over = jnp.where(scale * 1.02 + bias > CLAMP * LN2, 1.0, 0.0)
        over_own = jnp.where(scale * 1.02 - bias > CLAMP * LN2, 1.0, 0.0)
        sc = jnp.stack([scale * LOG2E, bias * LOG2E, over, over_own]).astype(F32)

        img_x = swap(img_own, X)
        txt_y = swap(txt_own, Y)
        txt_p = swap(txt_own, CORE)
        txt_yp = swap(txt_y, CORE)

        zero = jnp.zeros((rows, dim), F32)
        st = jnp.zeros((4, 8, 128), F32)
        back = dict(img_outer=False)

        tg_own, ig_own, st = block_call(sc, img_own, txt_own, zero, None, st, diag=True, irange=(0, 1), fresh_from=0)
        ig_own, tg_p, st = block_call(sc, img_own, txt_p, ig_own, None, st, fresh_from=1, **back)
        ig_x, tg_y, st = block_call(sc, img_x, txt_y, zero, None, st, fresh_from=0, **back)
        ig_x, tg_yp, st = block_call(sc, img_x, txt_yp, ig_x, None, st, **back)
        ig_own, tg_yp, st = block_call(sc, img_own, txt_yp, ig_own, tg_yp, st, **back)
        from_yp = swap(tg_yp, CORE)
        tg_own, ig_x0, st = block_call(sc, img_x, txt_own, tg_own, ig_x, st, irange=(0, half), keep_rows=cut)
        tg_p, ig_x0, st = block_call(sc, img_x, txt_p, tg_p, ig_x0, st, irange=(0, half), keep_rows=cut)
        from_x0 = swap(ig_x0, X)
        ig_own, tg_y0, st = block_call(sc, img_own, txt_y, ig_own, tg_y, st, jrange=(0, half), keep_rows=cut, extra=from_yp, **back)
        from_y0 = swap(tg_y0, Y)
        tg_own, ig_x1, st = block_call(sc, img_x, txt_own, tg_own, ig_x, st, irange=(half, nb), keep_rows=cut, keep_off=half)
        tg_p, ig_x1, st = block_call(sc, img_x, txt_p, tg_p, ig_x1, st, irange=(half, nb), keep_rows=cut, keep_off=half)
        from_x1 = swap(ig_x1, X)
        from_p = swap(tg_p, CORE)
        ig_own, tg_y1, st = block_call(sc, img_own, txt_y, ig_own, tg_y, st, jrange=(half, nb), keep_rows=cut, keep_off=half, extra=from_yp, **back)
        from_y1 = swap(tg_y1, Y)
        tg_own, ig_own, st = block_call(sc, img_own, txt_own, tg_own, ig_own, st, diag=True, irange=(1, nb))

        factor = scale / n_total
        img_grad = (ig_own + jnp.concatenate([from_x0, from_x1])) * factor
        txt_grad = (tg_own + from_p + jnp.concatenate([from_y0, from_y1])) * factor
        sums = jnp.sum(st, axis=(1, 2))
        sums = lax.psum(jnp.stack([sums[0] * LN2 + sums[1], sums[2], sums[3]]), axis_name)
        return (sums[0:1] / n_total, img_grad, txt_grad, sums[2:3] * factor, sums[1:2] / n_total)

    return jax.shard_map(per_device, mesh=mesh, in_specs=(P(axis_name, None), P(axis_name, None), P(None), P(None)), out_specs=(P(None), P(axis_name, None), P(axis_name, None), P(None), P(None)), check_vma=False)
```

profile of v0, /device:TPU:0, one launch (start us, length us, event | category | flops | bytes accessed | tf_op | source)
XLA Modules:
  0.0 903.8 jit_solution(13338621029920974903)
XLA Ops:
  0.6 3.4 collective-permute-start.1
  4.0 1.5 collective-permute-start
  6.8 0.1 pad_maximum_fusion.refs_0_
  6.9 4.5 broadcast_in_dim.6.clone.refs_3_
  11.4 26.0 %pair_block.12 = (f32[4096,512]{1,0:T(8,128)}, f32[4096,512]{1,0:T(8,128)}, f32[4,8,128]{2,1,0:T(8,128)S(1)}) custom-call(f32[4]{0:T(128)S(1)} %pad_maximum_fusion.refs_0_, bf16[4096,512]{1,0:T(8,128)(2,1)S(1)} %copy-done, bf16[4096,512]{1,0:T(8,128)(2,1)} %refs_2_.7, ...), custom_call_target="tpu_custom_call", output_to_operand_aliasing={{0}: (3, {}), {2}: (4, {})} | custom-call | flops 12884901888 | bytes 41943040 | tf_op jit(solution)/shard_map/pair_block/pallas_call | solution.py:154
  37.4 57.3 %collective-permute-done.1.refs_2_ = bf16[4096,512]{1,0:T(8,128)(2,1)S(1)} collective-permute-done((bf16[4096,512]{1,0:T(8,128)(2,1)}, bf16[4096,512]{1,0:T(8,128)(2,1)S(1)}, u32[]{:S(2)}, u32[]{:S(2)}) %collective-permute-start.1) | collective-permute-done | bytes 4194336 | tf_op jit(solution)/shard_map/ppermute | solution.py:177
  94.8 80.3 %pair_block.13 = (f32[4096,512]{1,0:T(8,128)}, f32[4096,512]{1,0:T(8,128)}, f32[4,8,128]{2,1,0:T(8,128)S(1)}) custom-call(f32[4]{0:T(128)S(1)} %pad_maximum_fusion.refs_0_, bf16[4096,512]{1,0:T(8,128)(2,1)S(1)} %copy-done, bf16[4096,512]{1,0:T(8,128)(2,1)} %collective-permute-done.3.refs_2_, ...), custom_call_target="tpu_custom_call", output_to_operand_aliasing={{0}: (3, {}), {2}: (4, {})} | custom-call | flops 51539607552 | bytes 41943040 | tf_op jit(solution)/shard_map/pair_block/pallas_call | solution.py:154
  175.1 4.5 broadcast_in_dim.6.refs_3_
  179.6 79.1 %pair_block.14 = (f32[4096,512]{1,0:T(8,128)}, f32[4096,512]{1,0:T(8,128)}, f32[4,8,128]{2,1,0:T(8,128)S(1)}) custom-call(f32[4]{0:T(128)S(1)} %pad_maximum_fusion.refs_0_, bf16[4096,512]{1,0:T(8,128)(2,1)S(1)} %collective-permute-done.refs_1_, bf16[4096,512]{1,0:T(8,128)(2,1)} %copy-done.5, ...), custom_call_target="tpu_custom_call", output_to_operand_aliasing={{0}: (3, {}), {2}: (4, {})} | custom-call | flops 51539607552 | bytes 41943040 | tf_op jit(solution)/shard_map/pair_block/pallas_call | solution.py:154
  258.7 78.4 %pair_block.15 = (f32[4096,512]{1,0:T(8,128)}, f32[4096,512]{1,0:T(8,128)}, f32[4,8,128]{2,1,0:T(8,128)S(1)}) custom-call(f32[4]{0:T(128)S(1)} %pad_maximum_fusion.refs_0_, bf16[4096,512]{1,0:T(8,128)(2,1)S(1)} %collective-permute-done.refs_1_, bf16[4096,512]{1,0:T(8,128)(2,1)} %collective-permute-done.2.refs_2_, ...), custom_call_target="tpu_custom_call", output_to_operand_aliasing={{0}: (3, {}), {2}: (4, {})} | custom-call | flops 51539607552 | bytes 41943040 | tf_op jit(solution)/shard_map/pair_block/pallas_call | solution.py:154
  337.1 79.5 %pair_block.16 = (f32[4096,512]{1,0:T(8,128)}, f32[4096,512]{1,0:T(8,128)}, f32[4,8,128]{2,1,0:T(8,128)S(1)}) custom-call(f32[4]{0:T(128)S(1)} %pad_maximum_fusion.refs_0_, bf16[4096,512]{1,0:T(8,128)(2,1)S(1)} %copy-done, bf16[4096,512]{1,0:T(8,128)(2,1)} %collective-permute-done.2.refs_2_, ...), custom_call_target="tpu_custom_call", output_to_operand_aliasing={{0}: (3, {}), {1}: (4, {}), {2}: (5, {})} | custom-call | flops 51539607552 | bytes 41943040 | tf_op jit(solution)/shard_map/pair_block/pallas_call | solution.py:154
  416.6 42.0 %pair_block.17 = (f32[4096,512]{1,0:T(8,128)}, f32[2048,512]{1,0:T(8,128)}, f32[4,8,128]{2,1,0:T(8,128)S(1)}) custom-call(f32[4]{0:T(128)S(1)} %pad_maximum_fusion.refs_0_, bf16[4096,512]{1,0:T(8,128)(2,1)} %copy-done.2, bf16[4096,512]{1,0:T(8,128)(2,1)} %refs_2_.7, ...), custom_call_target="tpu_custom_call", output_to_operand_aliasing={{0}: (3, {}), {2}: (5, {})} | custom-call | flops 25769803776 | bytes 41943040 | tf_op jit(solution)/shard_map/pair_block/pallas_call | solution.py:154
  458.6 42.1 %pair_block.18 = (f32[4096,512]{1,0:T(8,128)}, f32[2048,512]{1,0:T(8,128)}, f32[4,8,128]{2,1,0:T(8,128)S(1)}) custom-call(f32[4]{0:T(128)S(1)} %pad_maximum_fusion.refs_0_, bf16[4096,512]{1,0:T(8,128)(2,1)} %copy-done.2, bf16[4096,512]{1,0:T(8,128)(2,1)} %collective-permute-done.3.refs_2_, ...), custom_call_target="tpu_custom_call", output_to_operand_aliasing={{0}: (3, {}), {1}: (4, {}), {2}: (5, {})} | custom-call | flops 25769803776 | bytes 41943040 | tf_op jit(solution)/shard_map/pair_block/pallas_call | solution.py:154
  500.7 3.2 copy-done.4
  504.0 42.8 %pair_block.19 = (f32[4096,512]{1,0:T(8,128)}, f32[2048,512]{1,0:T(8,128)}, f32[4,8,128]{2,1,0:T(8,128)S(1)}) custom-call(f32[4]{0:T(128)S(1)} %pad_maximum_fusion.refs_0_, bf16[4096,512]{1,0:T(8,128)(2,1)} %refs_1_.11, bf16[4096,512]{1,0:T(8,128)(2,1)} %copy-done.5, ...), custom_call_target="tpu_custom_call", output_to_operand_aliasing={{0}: (3, {}), {2}: (6, {})} | custom-call | flops 25769803776 | bytes 41943040 | tf_op jit(solution)/shard_map/pair_block/pallas_call | solution.py:154
  546.7 42.2 %pair_block.20 = (f32[4096,512]{1,0:T(8,128)}, f32[2048,512]{1,0:T(8,128)}, f32[4,8,128]{2,1,0:T(8,128)S(1)}) custom-call(f32[4]{0:T(128)S(1)} %pad_maximum_fusion.refs_0_, bf16[4096,512]{1,0:T(8,128)(2,1)} %copy-done.2, bf16[4096,512]{1,0:T(8,128)(2,1)} %refs_2_.7, ...), custom_call_target="tpu_custom_call", output_to_operand_aliasing={{0}: (3, {}), {2}: (5, {})} | custom-call | flops 25769803776 | bytes 41943040 | tf_op jit(solution)/shard_map/pair_block/pallas_call | solution.py:154
  589.0 42.0 %pair_block.21 = (f32[4096,512]{1,0:T(8,128)}, f32[2048,512]{1,0:T(8,128)}, f32[4,8,128]{2,1,0:T(8,128)S(1)}) custom-call(f32[4]{0:T(128)S(1)} %pad_maximum_fusion.refs_0_, bf16[4096,512]{1,0:T(8,128)(2,1)} %copy-done.2, bf16[4096,512]{1,0:T(8,128)(2,1)} %collective-permute-done.3.refs_2_, ...), custom_call_target="tpu_custom_call", output_to_operand_aliasing={{0}: (3, {}), {1}: (4, {}), {2}: (5, {})} | custom-call | flops 25769803776 | bytes 41943040 | tf_op jit(solution)/shard_map/pair_block/pallas_call | solution.py:154
  631.0 0.5 collective-permute-start.7
  631.5 1.6 collective-permute-start.5
  633.1 0.4 collective-permute-start.6
  633.5 43.2 %pair_block.22 = (f32[4096,512]{1,0:T(8,128)}, f32[2048,512]{1,0:T(8,128)}, f32[4,8,128]{2,1,0:T(8,128)S(1)}) custom-call(f32[4]{0:T(128)S(1)} %pad_maximum_fusion.refs_0_, bf16[4096,512]{1,0:T(8,128)(2,1)} %refs_1_.11, bf16[4096,512]{1,0:T(8,128)(2,1)} %copy-done.5, ...), custom_call_target="tpu_custom_call", output_to_operand_aliasing={{0}: (3, {}), {2}: (6, {})} | custom-call | flops 25769803776 | bytes 41943040 | tf_op jit(solution)/shard_map/pair_block/pallas_call | solution.py:154
  676.8 1.7 collective-permute-start.9
  678.4 0.3 collective-permute-start.8
  678.8 69.8 %pair_block.23 = (f32[4096,512]{1,0:T(8,128)}, f32[4096,512]{1,0:T(8,128)}, f32[4,8,128]{2,1,0:T(8,128)S(1)}) custom-call(f32[4]{0:T(128)S(1)} %pad_maximum_fusion.refs_0_, bf16[4096,512]{1,0:T(8,128)(2,1)S(1)} %copy-done.1, bf16[4096,512]{1,0:T(8,128)(2,1)} %refs_2_.7, ...), custom_call_target="tpu_custom_call", output_to_operand_aliasing={{0}: (3, {}), {1}: (4, {}), {2}: (5, {})} | custom-call | flops 38654705664 | bytes 41943040 | tf_op jit(solution)/shard_map/pair_block/pallas_call | solution.py:154
  748.6 0.1 reduce_sum.9
  748.8 0.6 fusion.3
  750.7 0.1 pad_maximum_fusion.1
  750.8 126.1 %psum.7 = f32[3]{0:T(128)S(1)} all-reduce(f32[3]{0:T(128)S(1)} %pad_maximum_fusion.1), channel_id=1, replica_groups=mesh['dp'=8] {'dp'}, use_global_device_ids=true, to_apply=%region_1.2 | all-reduce | flops 3 | bytes 24 | tf_op jit(solution)/shard_map/psum | solution.py:225
  876.8 0.6 fusion.2
  879.4 10.2 %fusion = f32[4096,512]{1,0:T(8,128)} fusion(f32[4096,512]{1,0:T(8,128)} %get-tuple-element.70, f32[2048,512]{1,0:T(8,128)} %collective-permute-done.6, f32[2048,512]{1,0:T(8,128)} %collective-permute-done.5, f32[]{:T(128)} %bitcast), kind=kLoop, calls=%fused_computation.1 | loop fusion | flops 6291456 | bytes 25165828 | tf_op jit(solution)/shard_map/mul | solution.py:222
  889.6 1.0 copy-done.3
  890.6 9.3 %fusion.1 = f32[4096,512]{1,0:T(8,128)} fusion(f32[2048,512]{1,0:T(8,128)} %collective-permute-done.9, f32[2048,512]{1,0:T(8,128)} %collective-permute-done.8, f32[4096,512]{1,0:T(8,128)S(1)} %copy-done.3, f32[4096,512]{1,0:T(8,128)} %collective-permute-done.7, f32[]{:T(128)} %bitcast), kind=kLoop, calls=%fused_computation.3 | loop fusion | flops 8388608 | bytes 33554436 | tf_op jit(solution)/shard_map/mul | solution.py:223
  (24 shorter events, 0.1 us)
Async XLA Ops:
  0.6 10.8 %copy-start = (bf16[4096,512]{1,0:T(8,128)(2,1)S(1)}, bf16[4096,512]{1,0:T(8,128)(2,1)}, u32[]{:S(2)}) copy-start(bf16[4096,512]{1,0:T(8,128)(2,1)} %refs_1_.11) | copy-start | bytes 12582916
  0.6 94.1 %collective-permute-start.1 = (bf16[4096,512]{1,0:T(8,128)(2,1)}, bf16[4096,512]{1,0:T(8,128)(2,1)S(1)}, u32[]{:S(2)}, u32[]{:S(2)}) collective-permute-start(bf16[4096,512]{1,0:T(8,128)(2,1)} %refs_2_.7), channel_id=1, source_target_pairs={{0,4},{1,5},{2,6},{3,7},{4,0},{5,1},{6,2},{7,3}} | collective-permute-start | bytes 12582920 | tf_op jit(solution)/shard_map/ppermute | solution.py:177
  4.0 90.8 %collective-permute-start.3 = (bf16[4096,512]{1,0:T(8,128)(2,1)}, bf16[4096,512]{1,0:T(8,128)(2,1)}, u32[]{:S(2)}, u32[]{:S(2)}) collective-permute-start(bf16[4096,512]{1,0:T(8,128)(2,1)} %refs_2_.7), channel_id=1, source_target_pairs={{0,1},{1,0},{2,3},{3,2},{4,5},{5,4},{6,7},{7,6}} | collective-permute-start | bytes 12582920 | tf_op jit(solution)/shard_map/ppermute | solution.py:177
  4.0 171.1 %collective-permute-start = (bf16[4096,512]{1,0:T(8,128)(2,1)}, bf16[4096,512]{1,0:T(8,128)(2,1)S(1)}, u32[]{:S(2)}, u32[]{:S(2)}) collective-permute-start(bf16[4096,512]{1,0:T(8,128)(2,1)} %refs_1_.11), channel_id=1, source_target_pairs={{0,2},{1,3},{2,0},{3,1},{4,6},{5,7},{6,4},{7,5}} | collective-permute-start | bytes 12582920 | tf_op jit(solution)/shard_map/ppermute | solution.py:177
  94.8 80.3 %copy-start.5 = (bf16[4096,512]{1,0:T(8,128)(2,1)}, bf16[4096,512]{1,0:T(8,128)(2,1)S(1)}, u32[]{:S(2)}) copy-start(bf16[4096,512]{1,0:T(8,128)(2,1)S(1)} %collective-permute-done.1.refs_2_) | copy-start | bytes 12582916
  94.8 163.9 %collective-permute-start.2 = (bf16[4096,512]{1,0:T(8,128)(2,1)S(1)}, bf16[4096,512]{1,0:T(8,128)(2,1)}, u32[]{:S(2)}, u32[]{:S(2)}) collective-permute-start(bf16[4096,512]{1,0:T(8,128)(2,1)S(1)} %collective-permute-done.1.refs_2_), channel_id=1, source_target_pairs={{0,1},{1,0},{2,3},{3,2},{4,5},{5,4},{6,7},{7,6}} | collective-permute-start | bytes 12582920 | tf_op jit(solution)/shard_map/ppermute | solution.py:177
  175.1 83.6 %copy-start.2 = (bf16[4096,512]{1,0:T(8,128)(2,1)}, bf16[4096,512]{1,0:T(8,128)(2,1)S(1)}, u32[]{:S(2)}) copy-start(bf16[4096,512]{1,0:T(8,128)(2,1)S(1)} %collective-permute-done.refs_1_) | copy-start | bytes 12582916
  416.6 84.2 %collective-permute-start.4 = (f32[4096,512]{1,0:T(8,128)}, f32[4096,512]{1,0:T(8,128)S(1)}, u32[]{:S(2)}, u32[]{:S(2)}) collective-permute-start(f32[4096,512]{1,0:T(8,128)} %get-tuple-element.55), channel_id=1, source_target_pairs={{0,1},{1,0},{2,3},{3,2},{4,5},{5,4},{6,7},{7,6}} | collective-permute-start | bytes 25165832 | tf_op jit(solution)/shard_map/ppermute | solution.py:177
  500.7 3.2 copy-start.4
  631.0 258.6 %collective-permute-start.7 = (f32[4096,512]{1,0:T(8,128)}, f32[4096,512]{1,0:T(8,128)}, u32[]{:S(2)}, u32[]{:S(2)}) collective-permute-start(f32[4096,512]{1,0:T(8,128)} %get-tuple-element.74), channel_id=1, source_target_pairs={{0,1},{1,0},{2,3},{3,2},{4,5},{5,4},{6,7},{7,6}} | collective-permute-start | bytes 25165832 | tf_op jit(solution)/shard_map/ppermute | solution.py:177
  631.5 247.9 %collective-permute-start.5 = (f32[2048,512]{1,0:T(8,128)}, f32[2048,512]{1,0:T(8,128)}, u32[]{:S(2)}, u32[]{:S(2)}) collective-permute-start(f32[2048,512]{1,0:T(8,128)} %get-tuple-element.71), channel_id=1, source_target_pairs={{0,2},{1,3},{2,0},{3,1},{4,6},{5,7},{6,4},{7,5}} | collective-permute-start | bytes 12582920 | tf_op jit(solution)/shard_map/ppermute | solution.py:177
  633.1 246.2 %collective-permute-start.6 = (f32[2048,512]{1,0:T(8,128)}, f32[2048,512]{1,0:T(8,128)}, u32[]{:S(2)}, u32[]{:S(2)}) collective-permute-start(f32[2048,512]{1,0:T(8,128)} %get-tuple-element.72), channel_id=1, source_target_pairs={{0,2},{1,3},{2,0},{3,1},{4,6},{5,7},{6,4},{7,5}} | collective-permute-start | bytes 12582920 | tf_op jit(solution)/shard_map/ppermute | solution.py:177
  633.5 45.3 %copy-start.1 = (bf16[4096,512]{1,0:T(8,128)(2,1)S(1)}, bf16[4096,512]{1,0:T(8,128)(2,1)}, u32[]{:S(2)}) copy-start(bf16[4096,512]{1,0:T(8,128)(2,1)} %refs_1_.11) | copy-start | bytes 12582916
  676.8 212.8 %collective-permute-start.9 = (f32[2048,512]{1,0:T(8,128)}, f32[2048,512]{1,0:T(8,128)}, u32[]{:S(2)}, u32[]{:S(2)}) collective-permute-start(f32[2048,512]{1,0:T(8,128)} %get-tuple-element.76), channel_id=1, source_target_pairs={{0,4},{1,5},{2,6},{3,7},{4,0},{5,1},{6,2},{7,3}} | collective-permute-start | bytes 12582920 | tf_op jit(solution)/shard_map/ppermute | solution.py:177
  678.4 211.2 %collective-permute-start.8 = (f32[2048,512]{1,0:T(8,128)}, f32[2048,512]{1,0:T(8,128)}, u32[]{:S(2)}, u32[]{:S(2)}) collective-permute-start(f32[2048,512]{1,0:T(8,128)} %get-tuple-element.75), channel_id=1, source_target_pairs={{0,4},{1,5},{2,6},{3,7},{4,0},{5,1},{6,2},{7,3}} | collective-permute-start | bytes 12582920 | tf_op jit(solution)/shard_map/ppermute | solution.py:177
  879.4 11.3 %copy-start.3 = (f32[4096,512]{1,0:T(8,128)S(1)}, f32[4096,512]{1,0:T(8,128)}, u32[]{:S(2)}) copy-start(f32[4096,512]{1,0:T(8,128)} %get-tuple-element.73) | copy-start | bytes 25165828
where the time goes:
time: 912 us; the launch traced here: 904 us
  Pallas kernels  668 us (73%)
  blocking collectives  126 us (14%)
  waiting for transfers between devices  57.4 us (6%)
  other arithmetic  19.8 us (2%)
  local copies, waits for them, and re-layouts  14.5 us (2%)
  starting transfers between devices  9.4 us (1%)
  between operations  9.15 us (1%)
    pallas_call x12, Pallas kernels, block_call(): pl.pallas_call(kernel, grid=grid, in_specs=in_specs, out_specs=[nspec(n0)...  668 us
    psum x1, blocking collectives, per_device(): lax.psum(jnp.stack([sums[0] * LN2 + sums[1], sums[2], sums[3]]), axis_name)  126 us
    ppermute x10, waiting for transfers between devices, swap(): return lax.ppermute(x, axis_name, [(d, d ^ bit) for d in range(n_dev)])  57.4 us
  transfers between devices with their start and end apart: 10, of which 1 were waited for; matrix products, arithmetic and copies ran while one was open for 2% of the time, Pallas kernels for 42%

commit v1 on v0

--- a/solution.py
+++ b/solution.py
@@ -49,13 +49,16 @@
     return c, log_part, rest_part
 
 
-def block_kernel(*refs, diag, img_outer, i0, j0, keep_init, extra, fresh_from):
+def block_kernel(*refs, diag, img_outer, i0, j0, stream_init, keep_init, extra, fresh_from, spare):
     it = iter(refs)
     sc_ref, img_ref, txt_ref = next(it), next(it), next(it)
-    stream_in = next(it)
+    stream_in = next(it) if stream_init else None
     keep_in = next(it) if keep_init else None
     keep_extra = next(it) if extra else None
-    st_in, stream_ref, keep_ref, st_ref, coef = it
+    st_in, stream_ref, keep_ref, st_ref = next(it), next(it), next(it), next(it)
+    if spare:
+        next(it)
+    coef = next(it)
     outer, inner = pl.program_id(0), pl.program_id(1)
     i, j = (outer, inner) if img_outer else (inner, outer)
     s2 = sc_ref[0]
@@ -85,6 +88,11 @@
         col = lax.broadcasted_iota(jnp.int32, (rows, cols), 1) + ((j0 + j) * TILE + n)
         return row == col
 
+    def txt_part(n, k):
+        add = dot(coef[:, n:n + PIECE_N], img_ref[:, k:k + 256], TN)
+        tg_ref[n:n + PIECE_N, k:k + 256] = add if tg_base is None else tg_base[n:n + PIECE_N, k:k + 256] + add
+
+    queue = []
     for n in range(0, TILE, PIECE_N):
         for m in range(0, TILE, PIECE_M):
             dots = dot(img_ref[m:m + PIECE_M, :], txt_ref[n:n + PIECE_N, :], NT)
@@ -95,7 +103,12 @@
             st_ref[1] += fold(rest_part)
             st_ref[2] += fold(c)
             st_ref[3] += fold(c * dots)
-        tg_ref[n:n + PIECE_N, :] = tg_base[n:n + PIECE_N, :] + dot(coef[:, n:n + PIECE_N], img_ref[...], TN)
+            left = (TILE - m) // PIECE_M
+            for _ in range((len(queue) + left - 1) // left):
+                queue.pop(0)()
+        queue += [functools.partial(txt_part, n, k) for k in range(0, img_ref.shape[1], 256)]
+    for task in queue:
+        task()
     ig_ref[...] = ig_base[...] + dot(coef[...], txt_ref[...], NN)
 
     @pl.when(sc_ref[2] > 0.0)
@@ -116,7 +129,7 @@
             st_ref[0] += fold(jnp.broadcast_to(excess, (TILE, 128))) * (1.0 / 128.0)
 
 
-def block_call(sc, img, txt, stream, keep, st, *, diag=False, img_outer=True, irange=None, jrange=None, keep_off=0, keep_rows=None, extra=None, fresh_from=None):
+def block_call(sc, img, txt, stream, keep, st, *, diag=False, img_outer=True, irange=None, jrange=None, keep_off=0, keep_rows=None, extra=None, fresh_from=None, spare=False):
     dim = img.shape[1]
     i0, i1 = irange or (0, img.shape[0] // TILE)
     j0, j1 = jrange or (0, txt.shape[0] // TILE)
@@ -131,9 +144,12 @@
     sspec = pl.BlockSpec(st.shape, lambda a, b: (0, 0, 0))
     in_specs = [pl.BlockSpec(memory_space=pltpu.SMEM)]
     in_specs += [ospec(i0), nspec(j0)] if img_outer else [nspec(i0), ospec(j0)]
-    in_specs += [nspec(n0)]
-    args = [sc, img, txt, stream]
-    alias = {3: 0}
+    args = [sc, img, txt]
+    alias = {}
+    if stream is not None:
+        alias[len(args)] = 0
+        args.append(stream)
+        in_specs.append(nspec(n0))
     out_off = o0 - keep_off
     if keep is not None:
         in_off = o0 if keep.shape[0] > keep_rows else out_off
@@ -149,21 +165,25 @@
     in_specs.append(sspec)
     pairs = ni * nj * TILE * TILE
     kernel = functools.partial(
-        block_kernel, diag=diag, img_outer=img_outer, i0=i0, j0=j0, keep_init=keep is not None, extra=extra is not None, fresh_from=fresh_from
+        block_kernel, diag=diag, img_outer=img_outer, i0=i0, j0=j0, stream_init=stream is not None,
+        keep_init=keep is not None, extra=extra is not None, fresh_from=fresh_from, spare=spare,
     )
+    stream_shape = jax.ShapeDtypeStruct((txt if img_outer else img).shape, F32)
+    spare_specs = [pl.BlockSpec(memory_space=pl.ANY)] if spare else []
+    spare_shapes = [stream_shape] if spare else []
     return pl.pallas_call(
         kernel,
         grid=grid,
         in_specs=in_specs,
-        out_specs=[nspec(n0), ospec(out_off), sspec],
+        out_specs=[nspec(n0), ospec(out_off), sspec] + spare_specs,
         out_shape=[
-            jax.ShapeDtypeStruct(stream.shape, F32),
+            stream_shape,
             jax.ShapeDtypeStruct((keep_rows, dim), F32),
             jax.ShapeDtypeStruct(st.shape, F32),
-        ],
+        ] + spare_shapes,
         scratch_shapes=[pltpu.VMEM((TILE, TILE), BF16)],
         input_output_aliases=alias,
-        compiler_params=pltpu.CompilerParams(dimension_semantics=("arbitrary", "arbitrary"), vmem_limit_bytes=48 * 2**20),
+        compiler_params=pltpu.CompilerParams(dimension_semantics=("arbitrary", "arbitrary"), vmem_limit_bytes=63 * 2**20),
         cost_estimate=pl.CostEstimate(flops=6 * pairs * dim, transcendentals=3 * pairs, bytes_accessed=40 * 2**20),
         name="pair_block",
     )(*args)
@@ -179,7 +199,7 @@
     CORE, X, Y = 1, 2, 4
 
     def per_device(img_own, txt_own, log_temp, logit_bias):
-        rows, dim = img_own.shape
+        rows, _ = img_own.shape
         n_total = rows * n_dev
         nb = rows // TILE
         half = nb // 2
@@ -195,13 +215,12 @@
         txt_p = swap(txt_own, CORE)
         txt_yp = swap(txt_y, CORE)
 
-        zero = jnp.zeros((rows, dim), F32)
         st = jnp.zeros((4, 8, 128), F32)
         back = dict(img_outer=False)
 
-        tg_own, ig_own, st = block_call(sc, img_own, txt_own, zero, None, st, diag=True, irange=(0, 1), fresh_from=0)
+        tg_own, ig_own, st, spare = block_call(sc, img_own, txt_own, None, None, st, diag=True, irange=(0, 1), spare=True)
         ig_own, tg_p, st = block_call(sc, img_own, txt_p, ig_own, None, st, fresh_from=1, **back)
-        ig_x, tg_y, st = block_call(sc, img_x, txt_y, zero, None, st, fresh_from=0, **back)
+        ig_x, tg_y, st = block_call(sc, img_x, txt_y, spare, None, st, fresh_from=0, **back)
         ig_x, tg_yp, st = block_call(sc, img_x, txt_yp, ig_x, None, st, **back)
         ig_own, tg_yp, st = block_call(sc, img_own, txt_yp, ig_own, tg_yp, st, **back)
         from_yp = swap(tg_yp, CORE)
@@ -214,13 +233,16 @@
         tg_p, ig_x1, st = block_call(sc, img_x, txt_p, tg_p, ig_x1, st, irange=(half, nb), keep_rows=cut, keep_off=half)
         from_x1 = swap(ig_x1, X)
         from_p = swap(tg_p, CORE)
-        ig_own, tg_y1, st = block_call(sc, img_own, txt_y, ig_own, tg_y, st, jrange=(half, nb), keep_rows=cut, keep_off=half, extra=from_yp, **back)
+        last = cut - TILE
+        ig_own, tg_y1, st = block_call(sc, img_own, txt_y, ig_own, tg_y, st, jrange=(half, nb - 1), keep_rows=last, keep_off=half, extra=from_yp, **back)
         from_y1 = swap(tg_y1, Y)
+        ig_own, tg_y2, st = block_call(sc, img_own, txt_y, ig_own, tg_y, st, jrange=(nb - 1, nb), keep_rows=TILE, keep_off=nb - 1, extra=from_yp, **back)
+        from_y2 = swap(tg_y2, Y)
         tg_own, ig_own, st = block_call(sc, img_own, txt_own, tg_own, ig_own, st, diag=True, irange=(1, nb))
 
         factor = scale / n_total
         img_grad = (ig_own + jnp.concatenate([from_x0, from_x1])) * factor
-        txt_grad = (tg_own + from_p + jnp.concatenate([from_y0, from_y1])) * factor
+        txt_grad = (tg_own + from_p + jnp.concatenate([from_y0, from_y1, from_y2])) * factor
         sums = jnp.sum(st, axis=(1, 2))
         sums = lax.psum(jnp.stack([sums[0] * LN2 + sums[1], sums[2], sums[3]]), axis_name)
         return (sums[0:1] / n_total, img_grad, txt_grad, sums[2:3] * factor, sums[1:2] / n_total)

time: 912 us -> 877 us (0.962)
  Pallas kernels: 668 us -> 634 us
  local copies, waits for them, and re-layouts: 14.5 us -> 2.88 us
    pallas_call x12 -> x13, Pallas kernels: 668 us -> 634 us  [block_call(): pl.pallas_call(kernel, grid=grid, in_specs=in_specs, out_specs=[nspec(n0)...]
    ppermute x10 -> x11, waiting for transfers between devices: 57.4 us -> 63.1 us  [swap(): return lax.ppermute(x, axis_name, [(d, d ^ bit) for d in range(n_dev)])]
  transfers between devices with their start and end apart: 10 -> 11, of which waited for: 1 -> 1; matrix products, arithmetic and copies ran while one was open for 2% -> 2% of each run, Pallas kernels for 42% -> 56%
where the time goes in v1:
time: 877 us; the launch traced here: 869 us
  Pallas kernels  634 us (72%)
  blocking collectives  127 us (14%)
  waiting for transfers between devices  63.1 us (7%)
  other arithmetic  21.5 us (2%)
  starting transfers between devices  11.2 us (1%)
  between operations  8.93 us (1%)
    pallas_call x13, Pallas kernels, block_call(): pl.pallas_call(kernel, grid=grid, in_specs=in_specs, out_specs=[nspec(n0)...  634 us
    psum x1, blocking collectives, per_device(): lax.psum(jnp.stack([sums[0] * LN2 + sums[1], sums[2], sums[3]]), axis_name)  127 us
    ppermute x11, waiting for transfers between devices, swap(): return lax.ppermute(x, axis_name, [(d, d ^ bit) for d in range(n_dev)])  63.1 us
  transfers between devices with their start and end apart: 11, of which 1 were waited for; matrix products, arithmetic and copies ran while one was open for 2% of the time, Pallas kernels for 56%

profile of v1, /device:TPU:0, one launch (start us, length us, event | category | flops | bytes accessed | tf_op | source)
XLA Modules:
  0.0 869.1 jit_solution(11342805372502310306)
XLA Ops:
  0.6 3.4 collective-permute-start.1
  4.0 1.5 collective-permute-start
  6.8 0.6 pad_maximum_fusion.refs_0_
  7.4 0.6 broadcast_in_dim.3.refs_3_
  8.0 23.8 %pair_block.13 = (f32[4096,512]{1,0:T(8,128)}, f32[4096,512]{1,0:T(8,128)}, f32[4,8,128]{2,1,0:T(8,128)}, f32[4096,512]{1,0:T(8,128)}) custom-call(f32[4]{0:T(128)} %pad_maximum_fusion.refs_0_, bf16[4096,512]{1,0:T(8,128)(2,1)} %refs_1_.13, bf16[4096,512]{1,0:T(8,128)(2,1)} %refs_2_.7, ...), custom_call_target="tpu_custom_call", output_to_operand_aliasing={{2}: (3, {})} | custom-call | flops 12884901888 | bytes 41943040 | tf_op jit(solution)/shard_map/pair_block/pallas_call | solution.py:174
  31.8 63.0 %collective-permute-done.1.refs_2_ = bf16[4096,512]{1,0:T(8,128)(2,1)} collective-permute-done((bf16[4096,512]{1,0:T(8,128)(2,1)}, bf16[4096,512]{1,0:T(8,128)(2,1)}, u32[]{:S(2)}, u32[]{:S(2)}) %collective-permute-start.1) | collective-permute-done | bytes 4194336 | tf_op jit(solution)/shard_map/ppermute | solution.py:197
  94.9 74.2 %pair_block.14 = (f32[4096,512]{1,0:T(8,128)}, f32[4096,512]{1,0:T(8,128)}, f32[4,8,128]{2,1,0:T(8,128)}) custom-call(f32[4]{0:T(128)} %pad_maximum_fusion.refs_0_, bf16[4096,512]{1,0:T(8,128)(2,1)} %refs_1_.13, bf16[4096,512]{1,0:T(8,128)(2,1)} %collective-permute-done.3.refs_2_, ...), custom_call_target="tpu_custom_call", output_to_operand_aliasing={{0}: (3, {}), {2}: (4, {})} | custom-call | flops 51539607552 | bytes 41943040 | tf_op jit(solution)/shard_map/pair_block/pallas_call | solution.py:174
  169.1 74.7 %pair_block.15 = (f32[4096,512]{1,0:T(8,128)}, f32[4096,512]{1,0:T(8,128)}, f32[4,8,128]{2,1,0:T(8,128)}) custom-call(f32[4]{0:T(128)} %pad_maximum_fusion.refs_0_, bf16[4096,512]{1,0:T(8,128)(2,1)} %collective-permute-done.refs_1_, bf16[4096,512]{1,0:T(8,128)(2,1)} %collective-permute-done.1.refs_2_, ...), custom_call_target="tpu_custom_call", output_to_operand_aliasing={{0}: (3, {}), {2}: (4, {})} | custom-call | flops 51539607552 | bytes 41943040 | tf_op jit(solution)/shard_map/pair_block/pallas_call | solution.py:174
  243.8 73.7 %pair_block.16 = (f32[4096,512]{1,0:T(8,128)}, f32[4096,512]{1,0:T(8,128)}, f32[4,8,128]{2,1,0:T(8,128)}) custom-call(f32[4]{0:T(128)} %pad_maximum_fusion.refs_0_, bf16[4096,512]{1,0:T(8,128)(2,1)} %collective-permute-done.refs_1_, bf16[4096,512]{1,0:T(8,128)(2,1)} %collective-permute-done.2.refs_2_, ...), custom_call_target="tpu_custom_call", output_to_operand_aliasing={{0}: (3, {}), {2}: (4, {})} | custom-call | flops 51539607552 | bytes 41943040 | tf_op jit(solution)/shard_map/pair_block/pallas_call | solution.py:174
  317.6 74.8 %pair_block.17 = (f32[4096,512]{1,0:T(8,128)}, f32[4096,512]{1,0:T(8,128)}, f32[4,8,128]{2,1,0:T(8,128)}) custom-call(f32[4]{0:T(128)} %pad_maximum_fusion.refs_0_, bf16[4096,512]{1,0:T(8,128)(2,1)} %refs_1_.13, bf16[4096,512]{1,0:T(8,128)(2,1)} %collective-permute-done.2.refs_2_, ...), custom_call_target="tpu_custom_call", output_to_operand_aliasing={{0}: (3, {}), {1}: (4, {}), {2}: (5, {})} | custom-call | flops 51539607552 | bytes 41943040 | tf_op jit(solution)/shard_map/pair_block/pallas_call | solution.py:174
  392.4 0.5 collective-permute-start.4
  392.9 39.7 %pair_block.18 = (f32[4096,512]{1,0:T(8,128)}, f32[2048,512]{1,0:T(8,128)}, f32[4,8,128]{2,1,0:T(8,128)}) custom-call(f32[4]{0:T(128)} %pad_maximum_fusion.refs_0_, bf16[4096,512]{1,0:T(8,128)(2,1)} %collective-permute-done.refs_1_, bf16[4096,512]{1,0:T(8,128)(2,1)} %refs_2_.7, ...), custom_call_target="tpu_custom_call", output_to_operand_aliasing={{0}: (3, {}), {2}: (5, {})} | custom-call | flops 25769803776 | bytes 41943040 | tf_op jit(solution)/shard_map/pair_block/pallas_call | solution.py:174
  432.6 40.0 %pair_block.19 = (f32[4096,512]{1,0:T(8,128)}, f32[2048,512]{1,0:T(8,128)}, f32[4,8,128]{2,1,0:T(8,128)}) custom-call(f32[4]{0:T(128)} %pad_maximum_fusion.refs_0_, bf16[4096,512]{1,0:T(8,128)(2,1)} %collective-permute-done.refs_1_, bf16[4096,512]{1,0:T(8,128)(2,1)} %collective-permute-done.3.refs_2_, ...), custom_call_target="tpu_custom_call", output_to_operand_aliasing={{0}: (3, {}), {1}: (4, {}), {2}: (5, {})} | custom-call | flops 25769803776 | bytes 41943040 | tf_op jit(solution)/shard_map/pair_block/pallas_call | solution.py:174
  472.5 1.7 collective-permute-start.5
  474.3 40.5 %pair_block.20 = (f32[4096,512]{1,0:T(8,128)}, f32[2048,512]{1,0:T(8,128)}, f32[4,8,128]{2,1,0:T(8,128)}) custom-call(f32[4]{0:T(128)} %pad_maximum_fusion.refs_0_, bf16[4096,512]{1,0:T(8,128)(2,1)} %refs_1_.13, bf16[4096,512]{1,0:T(8,128)(2,1)} %collective-permute-done.1.refs_2_, ...), custom_call_target="tpu_custom_call", output_to_operand_aliasing={{0}: (3, {}), {2}: (6, {})} | custom-call | flops 25769803776 | bytes 41943040 | tf_op jit(solution)/shard_map/pair_block/pallas_call | solution.py:174
  514.8 40.2 %pair_block.21 = (f32[4096,512]{1,0:T(8,128)}, f32[2048,512]{1,0:T(8,128)}, f32[4,8,128]{2,1,0:T(8,128)}) custom-call(f32[4]{0:T(128)} %pad_maximum_fusion.refs_0_, bf16[4096,512]{1,0:T(8,128)(2,1)} %collective-permute-done.refs_1_, bf16[4096,512]{1,0:T(8,128)(2,1)} %refs_2_.7, ...), custom_call_target="tpu_custom_call", output_to_operand_aliasing={{0}: (3, {}), {2}: (5, {})} | custom-call | flops 25769803776 | bytes 41943040 | tf_op jit(solution)/shard_map/pair_block/pallas_call | solution.py:174
  555.0 39.8 %pair_block.22 = (f32[4096,512]{1,0:T(8,128)}, f32[2048,512]{1,0:T(8,128)}, f32[4,8,128]{2,1,0:T(8,128)}) custom-call(f32[4]{0:T(128)} %pad_maximum_fusion.refs_0_, bf16[4096,512]{1,0:T(8,128)(2,1)} %collective-permute-done.refs_1_, bf16[4096,512]{1,0:T(8,128)(2,1)} %collective-permute-done.3.refs_2_, ...), custom_call_target="tpu_custom_call", output_to_operand_aliasing={{0}: (3, {}), {1}: (4, {}), {2}: (5, {})} | custom-call | flops 25769803776 | bytes 41943040 | tf_op jit(solution)/shard_map/pair_block/pallas_call | solution.py:174
  594.8 0.3 collective-permute-start.6
  595.1 23.0 %pair_block.23 = (f32[4096,512]{1,0:T(8,128)}, f32[1024,512]{1,0:T(8,128)}, f32[4,8,128]{2,1,0:T(8,128)}) custom-call(f32[4]{0:T(128)} %pad_maximum_fusion.refs_0_, bf16[4096,512]{1,0:T(8,128)(2,1)} %refs_1_.13, bf16[4096,512]{1,0:T(8,128)(2,1)} %collective-permute-done.1.refs_2_, ...), custom_call_target="tpu_custom_call", output_to_operand_aliasing={{0}: (3, {}), {2}: (6, {})} | custom-call | flops 12884901888 | bytes 41943040 | tf_op jit(solution)/shard_map/pair_block/pallas_call | solution.py:174
  618.2 22.9 %pair_block.24 = (f32[4096,512]{1,0:T(8,128)}, f32[1024,512]{1,0:T(8,128)}, f32[4,8,128]{2,1,0:T(8,128)}) custom-call(f32[4]{0:T(128)} %pad_maximum_fusion.refs_0_, bf16[4096,512]{1,0:T(8,128)(2,1)} %refs_1_.13, bf16[4096,512]{1,0:T(8,128)(2,1)} %collective-permute-done.1.refs_2_, ...), custom_call_target="tpu_custom_call", output_to_operand_aliasing={{0}: (3, {}), {2}: (6, {})} | custom-call | flops 12884901888 | bytes 41943040 | tf_op jit(solution)/shard_map/pair_block/pallas_call | solution.py:174
  641.1 1.8 collective-permute-start.10
  642.8 0.3 collective-permute-start.9
  643.1 1.7 collective-permute-start.8
  644.9 66.9 %pair_block.25 = (f32[4096,512]{1,0:T(8,128)}, f32[4096,512]{1,0:T(8,128)}, f32[4,8,128]{2,1,0:T(8,128)}) custom-call(f32[4]{0:T(128)} %pad_maximum_fusion.refs_0_, bf16[4096,512]{1,0:T(8,128)(2,1)} %refs_1_.13, bf16[4096,512]{1,0:T(8,128)(2,1)} %refs_2_.7, ...), custom_call_target="tpu_custom_call", output_to_operand_aliasing={{0}: (3, {}), {1}: (4, {}), {2}: (5, {})} | custom-call | flops 38654705664 | bytes 41943040 | tf_op jit(solution)/shard_map/pair_block/pallas_call | solution.py:174
  711.8 0.8 reduce_sum.9
  712.7 0.6 fusion.3
  714.5 0.1 pad_maximum_fusion.1
  714.6 127.3 %psum.7 = f32[3]{0:T(128)S(1)} all-reduce(f32[3]{0:T(128)S(1)} %pad_maximum_fusion.1), channel_id=1, replica_groups=mesh['dp'=8] {'dp'}, use_global_device_ids=true, to_apply=%region_1.2 | all-reduce | flops 3 | bytes 24 | tf_op jit(solution)/shard_map/psum | solution.py:247
  842.0 0.6 fusion.2
  844.5 10.2 %fusion = f32[4096,512]{1,0:T(8,128)} fusion(f32[4096,512]{1,0:T(8,128)} %get-tuple-element.77, f32[2048,512]{1,0:T(8,128)} %collective-permute-done.6, f32[2048,512]{1,0:T(8,128)} %collective-permute-done.5, f32[]{:T(128)} %bitcast), kind=kLoop, calls=%fused_computation.1 | loop fusion | flops 6291456 | bytes 25165828 | tf_op jit(solution)/shard_map/mul | solution.py:244
  854.7 1.0 copy-done
  855.8 9.8 %fusion.1 = f32[4096,512]{1,0:T(8,128)} fusion(f32[1024,512]{1,0:T(8,128)} %collective-permute-done.10, f32[1024,512]{1,0:T(8,128)} %collective-permute-done.9, f32[2048,512]{1,0:T(8,128)} %collective-permute-done.8, f32[4096,512]{1,0:T(8,128)S(1)} %copy-done, f32[4096,512]{1,0:T(8,128)} %collective-permute-done.7, f32[]{:T(128)} %bitcast), kind=kLoop, calls=%fused_computation.3 | loop fusion | flops 10485760 | bytes 33554436 | tf_op jit(solution)/shard_map/mul | solution.py:245
  (15 shorter events, 0.1 us)
Async XLA Ops:
  0.6 94.2 %collective-permute-start.1 = (bf16[4096,512]{1,0:T(8,128)(2,1)}, bf16[4096,512]{1,0:T(8,128)(2,1)}, u32[]{:S(2)}, u32[]{:S(2)}) collective-permute-start(bf16[4096,512]{1,0:T(8,128)(2,1)} %refs_2_.7), channel_id=1, source_target_pairs={{0,4},{1,5},{2,6},{3,7},{4,0},{5,1},{6,2},{7,3}} | collective-permute-start | bytes 12582920 | tf_op jit(solution)/shard_map/ppermute | solution.py:197
  4.0 90.9 %collective-permute-start.3 = (bf16[4096,512]{1,0:T(8,128)(2,1)}, bf16[4096,512]{1,0:T(8,128)(2,1)}, u32[]{:S(2)}, u32[]{:S(2)}) collective-permute-start(bf16[4096,512]{1,0:T(8,128)(2,1)} %refs_2_.7), channel_id=1, source_target_pairs={{0,1},{1,0},{2,3},{3,2},{4,5},{5,4},{6,7},{7,6}} | collective-permute-start | bytes 12582920 | tf_op jit(solution)/shard_map/ppermute | solution.py:197
  4.0 165.1 %collective-permute-start = (bf16[4096,512]{1,0:T(8,128)(2,1)}, bf16[4096,512]{1,0:T(8,128)(2,1)}, u32[]{:S(2)}, u32[]{:S(2)}) collective-permute-start(bf16[4096,512]{1,0:T(8,128)(2,1)} %refs_1_.13), channel_id=1, source_target_pairs={{0,2},{1,3},{2,0},{3,1},{4,6},{5,7},{6,4},{7,5}} | collective-permute-start | bytes 12582920 | tf_op jit(solution)/shard_map/ppermute | solution.py:197
  94.9 149.0 %collective-permute-start.2 = (bf16[4096,512]{1,0:T(8,128)(2,1)}, bf16[4096,512]{1,0:T(8,128)(2,1)}, u32[]{:S(2)}, u32[]{:S(2)}) collective-permute-start(bf16[4096,512]{1,0:T(8,128)(2,1)} %collective-permute-done.1.refs_2_), channel_id=1, source_target_pairs={{0,1},{1,0},{2,3},{3,2},{4,5},{5,4},{6,7},{7,6}} | collective-permute-start | bytes 12582920 | tf_op jit(solution)/shard_map/ppermute | solution.py:197
  392.4 81.9 %collective-permute-start.4 = (f32[4096,512]{1,0:T(8,128)}, f32[4096,512]{1,0:T(8,128)}, u32[]{:S(2)}, u32[]{:S(2)}) collective-permute-start(f32[4096,512]{1,0:T(8,128)} %get-tuple-element.60), channel_id=1, source_target_pairs={{0,1},{1,0},{2,3},{3,2},{4,5},{5,4},{6,7},{7,6}} | collective-permute-start | bytes 25165832 | tf_op jit(solution)/shard_map/ppermute | solution.py:197
  472.5 170.6 %collective-permute-start.5 = (f32[2048,512]{1,0:T(8,128)}, f32[2048,512]{1,0:T(8,128)}, u32[]{:S(2)}, u32[]{:S(2)}) collective-permute-start(f32[2048,512]{1,0:T(8,128)} %get-tuple-element.78), channel_id=1, source_target_pairs={{0,2},{1,3},{2,0},{3,1},{4,6},{5,7},{6,4},{7,5}} | collective-permute-start | bytes 12582920 | tf_op jit(solution)/shard_map/ppermute | solution.py:197
  594.8 260.0 %collective-permute-start.7 = (f32[4096,512]{1,0:T(8,128)}, f32[4096,512]{1,0:T(8,128)}, u32[]{:S(2)}, u32[]{:S(2)}) collective-permute-start(f32[4096,512]{1,0:T(8,128)} %get-tuple-element.81), channel_id=1, source_target_pairs={{0,1},{1,0},{2,3},{3,2},{4,5},{5,4},{6,7},{7,6}} | collective-permute-start | bytes 25165832 | tf_op jit(solution)/shard_map/ppermute | solution.py:197
  594.8 249.7 %collective-permute-start.6 = (f32[2048,512]{1,0:T(8,128)}, f32[2048,512]{1,0:T(8,128)}, u32[]{:S(2)}, u32[]{:S(2)}) collective-permute-start(f32[2048,512]{1,0:T(8,128)} %get-tuple-element.79), channel_id=1, source_target_pairs={{0,2},{1,3},{2,0},{3,1},{4,6},{5,7},{6,4},{7,5}} | collective-permute-start | bytes 12582920 | tf_op jit(solution)/shard_map/ppermute | solution.py:197
  641.1 213.6 %collective-permute-start.10 = (f32[1024,512]{1,0:T(8,128)}, f32[1024,512]{1,0:T(8,128)}, u32[]{:S(2)}, u32[]{:S(2)}) collective-permute-start(f32[1024,512]{1,0:T(8,128)} %get-tuple-element.84), channel_id=1, source_target_pairs={{0,4},{1,5},{2,6},{3,7},{4,0},{5,1},{6,2},{7,3}} | collective-permute-start | bytes 6291464 | tf_op jit(solution)/shard_map/ppermute | solution.py:197
  642.8 211.9 %collective-permute-start.9 = (f32[1024,512]{1,0:T(8,128)}, f32[1024,512]{1,0:T(8,128)}, u32[]{:S(2)}, u32[]{:S(2)}) collective-permute-start(f32[1024,512]{1,0:T(8,128)} %get-tuple-element.83), channel_id=1, source_target_pairs={{0,4},{1,5},{2,6},{3,7},{4,0},{5,1},{6,2},{7,3}} | collective-permute-start | bytes 6291464 | tf_op jit(solution)/shard_map/ppermute | solution.py:197
  643.1 211.6 %collective-permute-start.8 = (f32[2048,512]{1,0:T(8,128)}, f32[2048,512]{1,0:T(8,128)}, u32[]{:S(2)}, u32[]{:S(2)}) collective-permute-start(f32[2048,512]{1,0:T(8,128)} %get-tuple-element.82), channel_id=1, source_target_pairs={{0,4},{1,5},{2,6},{3,7},{4,0},{5,1},{6,2},{7,3}} | collective-permute-start | bytes 12582920 | tf_op jit(solution)/shard_map/ppermute | solution.py:197
  844.5 11.3 %copy-start = (f32[4096,512]{1,0:T(8,128)S(1)}, f32[4096,512]{1,0:T(8,128)}, u32[]{:S(2)}) copy-start(f32[4096,512]{1,0:T(8,128)} %get-tuple-element.80) | copy-start | bytes 25165828

commit v2 on v1

--- a/solution.py
+++ b/solution.py
@@ -92,24 +92,34 @@
         add = dot(coef[:, n:n + PIECE_N], img_ref[:, k:k + 256], TN)
         tg_ref[n:n + PIECE_N, k:k + 256] = add if tg_base is None else tg_base[n:n + PIECE_N, k:k + 256] + add
 
-    queue = []
-    for n in range(0, TILE, PIECE_N):
-        for m in range(0, TILE, PIECE_M):
-            dots = dot(img_ref[m:m + PIECE_M, :], txt_ref[n:n + PIECE_N, :], NT)
-            flip = flip_mask(m, n, PIECE_M, PIECE_N) if diag else None
-            c, log_part, rest_part = pair_terms(dots * s2 + b2, flip)
-            coef[m:m + PIECE_M, n:n + PIECE_N] = c.astype(BF16)
-            st_ref[0] += fold(log_part)
-            st_ref[1] += fold(rest_part)
-            st_ref[2] += fold(c)
-            st_ref[3] += fold(c * dots)
-            left = (TILE - m) // PIECE_M
-            for _ in range((len(queue) + left - 1) // left):
-                queue.pop(0)()
-        queue += [functools.partial(txt_part, n, k) for k in range(0, img_ref.shape[1], 256)]
-    for task in queue:
-        task()
-    ig_ref[...] = ig_base[...] + dot(coef[...], txt_ref[...], NN)
+    def tile(on_diag):
+        queue = []
+        for n in range(0, TILE, PIECE_N):
+            for m in range(0, TILE, PIECE_M):
+                dots = dot(img_ref[m:m + PIECE_M, :], txt_ref[n:n + PIECE_N, :], NT)
+                flip = None
+                if on_diag and m < n + PIECE_N and n < m + PIECE_M:
+                    shape = (PIECE_M, PIECE_N)
+                    flip = lax.broadcasted_iota(jnp.int32, shape, 0) + (m - n) == lax.broadcasted_iota(jnp.int32, shape, 1)
+                c, log_part, rest_part = pair_terms(dots * s2 + b2, flip)
+                coef[m:m + PIECE_M, n:n + PIECE_N] = c.astype(BF16)
+                st_ref[0] += fold(log_part)
+                st_ref[1] += fold(rest_part)
+                st_ref[2] += fold(c)
+                st_ref[3] += fold(c * dots)
+                left = (TILE - m) // PIECE_M
+                for _ in range((len(queue) + left - 1) // left):
+                    queue.pop(0)()
+            queue += [functools.partial(txt_part, n, k) for k in range(0, img_ref.shape[1], 256)]
+        for task in queue:
+            task()
+        ig_ref[...] = ig_base[...] + dot(coef[...], txt_ref[...], NN)
+
+    if diag:
+        pl.when(i0 + i == j0 + j)(lambda: tile(True))
+        pl.when(i0 + i != j0 + j)(lambda: tile(False))
+    else:
+        tile(False)
 
     @pl.when(sc_ref[2] > 0.0)
     def _():
@@ -224,13 +234,12 @@
         ig_x, tg_yp, st = block_call(sc, img_x, txt_yp, ig_x, None, st, **back)
         ig_own, tg_yp, st = block_call(sc, img_own, txt_yp, ig_own, tg_yp, st, **back)
         from_yp = swap(tg_yp, CORE)
-        tg_own, ig_x0, st = block_call(sc, img_x, txt_own, tg_own, ig_x, st, irange=(0, half), keep_rows=cut)
-        tg_p, ig_x0, st = block_call(sc, img_x, txt_p, tg_p, ig_x0, st, irange=(0, half), keep_rows=cut)
+        tg_own, ig_x, st = block_call(sc, img_x, txt_own, tg_own, ig_x, st)
+        tg_p, ig_x0, st = block_call(sc, img_x, txt_p, tg_p, ig_x, st, irange=(0, half), keep_rows=cut)
         from_x0 = swap(ig_x0, X)
         ig_own, tg_y0, st = block_call(sc, img_own, txt_y, ig_own, tg_y, st, jrange=(0, half), keep_rows=cut, extra=from_yp, **back)
         from_y0 = swap(tg_y0, Y)
-        tg_own, ig_x1, st = block_call(sc, img_x, txt_own, tg_own, ig_x, st, irange=(half, nb), keep_rows=cut, keep_off=half)
-        tg_p, ig_x1, st = block_call(sc, img_x, txt_p, tg_p, ig_x1, st, irange=(half, nb), keep_rows=cut, keep_off=half)
+        tg_p, ig_x1, st = block_call(sc, img_x, txt_p, tg_p, ig_x, st, irange=(half, nb), keep_rows=cut, keep_off=half)
         from_x1 = swap(ig_x1, X)
         from_p = swap(tg_p, CORE)
         last = cut - TILE

time: 877 us -> 872 us (level)
  Pallas kernels: 634 us -> 625 us
    pallas_call x13 -> x12, Pallas kernels: 634 us -> 625 us  [block_call(): pl.pallas_call(kernel, grid=grid, in_specs=in_specs, out_specs=[nspec(n0)...]
  transfers between devices with their start and end apart: 11 -> 11, of which waited for: 1 -> 1; matrix products, arithmetic and copies ran while one was open for 2% -> 2% of each run, Pallas kernels for 56% -> 55%
where the time goes in v2:
time: 872 us; the launch traced here: 865 us
  Pallas kernels  625 us (72%)
  blocking collectives  131 us (15%)
  waiting for transfers between devices  64.1 us (7%)
  other arithmetic  21.5 us (2%)
  starting transfers between devices  11.2 us (1%)
  between operations  9.14 us (1%)
    pallas_call x12, Pallas kernels, block_call(): pl.pallas_call(kernel, grid=grid, in_specs=in_specs, out_specs=[nspec(n0)...  625 us
    psum x1, blocking collectives, per_device(): lax.psum(jnp.stack([sums[0] * LN2 + sums[1], sums[2], sums[3]]), axis_name)  131 us
    ppermute x11, waiting for transfers between devices, swap(): return lax.ppermute(x, axis_name, [(d, d ^ bit) for d in range(n_dev)])  64.1 us
  transfers between devices with their start and end apart: 11, of which 1 were waited for; matrix products, arithmetic and copies ran while one was open for 2% of the time, Pallas kernels for 55%

profile of v2, /device:TPU:0, one launch (start us, length us, event | category | flops | bytes accessed | tf_op | source)
XLA Modules:
  0.0 864.7 jit_solution(15832145664109716607)
XLA Ops:
  0.6 3.4 collective-permute-start.1
  4.0 1.5 collective-permute-start
  6.8 0.6 pad_maximum_fusion.refs_0_
  7.4 0.6 broadcast_in_dim.3.refs_3_
  8.0 22.8 %pair_block.12 = (f32[4096,512]{1,0:T(8,128)}, f32[4096,512]{1,0:T(8,128)}, f32[4,8,128]{2,1,0:T(8,128)}, f32[4096,512]{1,0:T(8,128)}) custom-call(f32[4]{0:T(128)} %pad_maximum_fusion.refs_0_, bf16[4096,512]{1,0:T(8,128)(2,1)} %refs_1_.13, bf16[4096,512]{1,0:T(8,128)(2,1)} %refs_2_.5, ...), custom_call_target="tpu_custom_call", output_to_operand_aliasing={{2}: (3, {})} | custom-call | flops 12884901888 | bytes 41943040 | tf_op jit(solution)/shard_map/pair_block/pallas_call | solution.py:184
  30.8 64.1 %collective-permute-done.1.refs_2_ = bf16[4096,512]{1,0:T(8,128)(2,1)} collective-permute-done((bf16[4096,512]{1,0:T(8,128)(2,1)}, bf16[4096,512]{1,0:T(8,128)(2,1)}, u32[]{:S(2)}, u32[]{:S(2)}) %collective-permute-start.1) | collective-permute-done | bytes 4194336 | tf_op jit(solution)/shard_map/ppermute | solution.py:207
  94.9 74.5 %pair_block.13 = (f32[4096,512]{1,0:T(8,128)}, f32[4096,512]{1,0:T(8,128)}, f32[4,8,128]{2,1,0:T(8,128)}) custom-call(f32[4]{0:T(128)} %pad_maximum_fusion.refs_0_, bf16[4096,512]{1,0:T(8,128)(2,1)} %refs_1_.13, bf16[4096,512]{1,0:T(8,128)(2,1)} %collective-permute-done.3.refs_2_, ...), custom_call_target="tpu_custom_call", output_to_operand_aliasing={{0}: (3, {}), {2}: (4, {})} | custom-call | flops 51539607552 | bytes 41943040 | tf_op jit(solution)/shard_map/pair_block/pallas_call | solution.py:184
  169.4 74.5 %pair_block.14 = (f32[4096,512]{1,0:T(8,128)}, f32[4096,512]{1,0:T(8,128)}, f32[4,8,128]{2,1,0:T(8,128)}) custom-call(f32[4]{0:T(128)} %pad_maximum_fusion.refs_0_, bf16[4096,512]{1,0:T(8,128)(2,1)} %collective-permute-done.refs_1_, bf16[4096,512]{1,0:T(8,128)(2,1)} %collective-permute-done.1.refs_2_, ...), custom_call_target="tpu_custom_call", output_to_operand_aliasing={{0}: (3, {}), {2}: (4, {})} | custom-call | flops 51539607552 | bytes 41943040 | tf_op jit(solution)/shard_map/pair_block/pallas_call | solution.py:184
  243.9 74.0 %pair_block.15 = (f32[4096,512]{1,0:T(8,128)}, f32[4096,512]{1,0:T(8,128)}, f32[4,8,128]{2,1,0:T(8,128)}) custom-call(f32[4]{0:T(128)} %pad_maximum_fusion.refs_0_, bf16[4096,512]{1,0:T(8,128)(2,1)} %collective-permute-done.refs_1_, bf16[4096,512]{1,0:T(8,128)(2,1)} %collective-permute-done.2.refs_2_, ...), custom_call_target="tpu_custom_call", output_to_operand_aliasing={{0}: (3, {}), {2}: (4, {})} | custom-call | flops 51539607552 | bytes 41943040 | tf_op jit(solution)/shard_map/pair_block/pallas_call | solution.py:184
  317.9 74.6 %pair_block.16 = (f32[4096,512]{1,0:T(8,128)}, f32[4096,512]{1,0:T(8,128)}, f32[4,8,128]{2,1,0:T(8,128)}) custom-call(f32[4]{0:T(128)} %pad_maximum_fusion.refs_0_, bf16[4096,512]{1,0:T(8,128)(2,1)} %refs_1_.13, bf16[4096,512]{1,0:T(8,128)(2,1)} %collective-permute-done.2.refs_2_, ...), custom_call_target="tpu_custom_call", output_to_operand_aliasing={{0}: (3, {}), {1}: (4, {}), {2}: (5, {})} | custom-call | flops 51539607552 | bytes 41943040 | tf_op jit(solution)/shard_map/pair_block/pallas_call | solution.py:184
  392.4 0.5 collective-permute-start.4
  392.9 75.1 %pair_block.17 = (f32[4096,512]{1,0:T(8,128)}, f32[4096,512]{1,0:T(8,128)}, f32[4,8,128]{2,1,0:T(8,128)}) custom-call(f32[4]{0:T(128)} %pad_maximum_fusion.refs_0_, bf16[4096,512]{1,0:T(8,128)(2,1)} %collective-permute-done.refs_1_, bf16[4096,512]{1,0:T(8,128)(2,1)} %refs_2_.5, ...), custom_call_target="tpu_custom_call", output_to_operand_aliasing={{0}: (3, {}), {1}: (4, {}), {2}: (5, {})} | custom-call | flops 51539607552 | bytes 41943040 | tf_op jit(solution)/shard_map/pair_block/pallas_call | solution.py:184
  468.0 39.7 %pair_block.18 = (f32[4096,512]{1,0:T(8,128)}, f32[2048,512]{1,0:T(8,128)}, f32[4,8,128]{2,1,0:T(8,128)}) custom-call(f32[4]{0:T(128)} %pad_maximum_fusion.refs_0_, bf16[4096,512]{1,0:T(8,128)(2,1)} %collective-permute-done.refs_1_, bf16[4096,512]{1,0:T(8,128)(2,1)} %collective-permute-done.3.refs_2_, ...), custom_call_target="tpu_custom_call", output_to_operand_aliasing={{0}: (3, {}), {2}: (5, {})} | custom-call | flops 25769803776 | bytes 41943040 | tf_op jit(solution)/shard_map/pair_block/pallas_call | solution.py:184
  507.6 1.7 collective-permute-start.5
  509.4 40.7 %pair_block.19 = (f32[4096,512]{1,0:T(8,128)}, f32[2048,512]{1,0:T(8,128)}, f32[4,8,128]{2,1,0:T(8,128)}) custom-call(f32[4]{0:T(128)} %pad_maximum_fusion.refs_0_, bf16[4096,512]{1,0:T(8,128)(2,1)} %refs_1_.13, bf16[4096,512]{1,0:T(8,128)(2,1)} %collective-permute-done.1.refs_2_, ...), custom_call_target="tpu_custom_call", output_to_operand_aliasing={{0}: (3, {}), {2}: (6, {})} | custom-call | flops 25769803776 | bytes 41943040 | tf_op jit(solution)/shard_map/pair_block/pallas_call | solution.py:184
  550.1 39.9 %pair_block.20 = (f32[4096,512]{1,0:T(8,128)}, f32[2048,512]{1,0:T(8,128)}, f32[4,8,128]{2,1,0:T(8,128)}) custom-call(f32[4]{0:T(128)} %pad_maximum_fusion.refs_0_, bf16[4096,512]{1,0:T(8,128)(2,1)} %collective-permute-done.refs_1_, bf16[4096,512]{1,0:T(8,128)(2,1)} %collective-permute-done.3.refs_2_, ...), custom_call_target="tpu_custom_call", output_to_operand_aliasing={{0}: (3, {}), {2}: (5, {})} | custom-call | flops 25769803776 | bytes 41943040 | tf_op jit(solution)/shard_map/pair_block/pallas_call | solution.py:184
  590.0 0.3 collective-permute-start.6
  590.4 23.0 %pair_block.21 = (f32[4096,512]{1,0:T(8,128)}, f32[1024,512]{1,0:T(8,128)}, f32[4,8,128]{2,1,0:T(8,128)}) custom-call(f32[4]{0:T(128)} %pad_maximum_fusion.refs_0_, bf16[4096,512]{1,0:T(8,128)(2,1)} %refs_1_.13, bf16[4096,512]{1,0:T(8,128)(2,1)} %collective-permute-done.1.refs_2_, ...), custom_call_target="tpu_custom_call", output_to_operand_aliasing={{0}: (3, {}), {2}: (6, {})} | custom-call | flops 12884901888 | bytes 41943040 | tf_op jit(solution)/shard_map/pair_block/pallas_call | solution.py:184
  613.4 23.0 %pair_block.22 = (f32[4096,512]{1,0:T(8,128)}, f32[1024,512]{1,0:T(8,128)}, f32[4,8,128]{2,1,0:T(8,128)}) custom-call(f32[4]{0:T(128)} %pad_maximum_fusion.refs_0_, bf16[4096,512]{1,0:T(8,128)(2,1)} %refs_1_.13, bf16[4096,512]{1,0:T(8,128)(2,1)} %collective-permute-done.1.refs_2_, ...), custom_call_target="tpu_custom_call", output_to_operand_aliasing={{0}: (3, {}), {2}: (6, {})} | custom-call | flops 12884901888 | bytes 41943040 | tf_op jit(solution)/shard_map/pair_block/pallas_call | solution.py:184
  636.4 1.8 collective-permute-start.10
  638.1 0.3 collective-permute-start.9
  638.4 1.7 collective-permute-start.8
  640.2 63.7 %pair_block.23 = (f32[4096,512]{1,0:T(8,128)}, f32[4096,512]{1,0:T(8,128)}, f32[4,8,128]{2,1,0:T(8,128)}) custom-call(f32[4]{0:T(128)} %pad_maximum_fusion.refs_0_, bf16[4096,512]{1,0:T(8,128)(2,1)} %refs_1_.13, bf16[4096,512]{1,0:T(8,128)(2,1)} %refs_2_.5, ...), custom_call_target="tpu_custom_call", output_to_operand_aliasing={{0}: (3, {}), {1}: (4, {}), {2}: (5, {})} | custom-call | flops 38654705664 | bytes 41943040 | tf_op jit(solution)/shard_map/pair_block/pallas_call | solution.py:184
  703.9 0.8 reduce_sum.9
  704.7 0.1 slice.22
  704.8 0.6 fusion.3
  706.7 0.1 pad_maximum_fusion.1
  706.7 130.5 %psum.7 = f32[3]{0:T(128)S(1)} all-reduce(f32[3]{0:T(128)S(1)} %pad_maximum_fusion.1), channel_id=1, replica_groups=mesh['dp'=8] {'dp'}, use_global_device_ids=true, to_apply=%region_1.2 | all-reduce | flops 3 | bytes 24 | tf_op jit(solution)/shard_map/psum | solution.py:256
  837.3 0.6 fusion.2
  839.8 10.2 %fusion = f32[4096,512]{1,0:T(8,128)} fusion(f32[4096,512]{1,0:T(8,128)} %get-tuple-element.71, f32[2048,512]{1,0:T(8,128)} %collective-permute-done.6, f32[2048,512]{1,0:T(8,128)} %collective-permute-done.5, f32[]{:T(128)} %bitcast), kind=kLoop, calls=%fused_computation.1 | loop fusion | flops 6291456 | bytes 25165828 | tf_op jit(solution)/shard_map/mul | solution.py:253
  850.1 1.0 copy-done
  851.1 9.8 %fusion.1 = f32[4096,512]{1,0:T(8,128)} fusion(f32[1024,512]{1,0:T(8,128)} %collective-permute-done.10, f32[1024,512]{1,0:T(8,128)} %collective-permute-done.9, f32[2048,512]{1,0:T(8,128)} %collective-permute-done.8, f32[4096,512]{1,0:T(8,128)S(1)} %copy-done, f32[4096,512]{1,0:T(8,128)} %collective-permute-done.7, f32[]{:T(128)} %bitcast), kind=kLoop, calls=%fused_computation.3 | loop fusion | flops 10485760 | bytes 33554436 | tf_op jit(solution)/shard_map/mul | solution.py:254
  (14 shorter events, 0.1 us)
Async XLA Ops:
  0.6 94.2 %collective-permute-start.1 = (bf16[4096,512]{1,0:T(8,128)(2,1)}, bf16[4096,512]{1,0:T(8,128)(2,1)}, u32[]{:S(2)}, u32[]{:S(2)}) collective-permute-start(bf16[4096,512]{1,0:T(8,128)(2,1)} %refs_2_.5), channel_id=1, source_target_pairs={{0,4},{1,5},{2,6},{3,7},{4,0},{5,1},{6,2},{7,3}} | collective-permute-start | bytes 12582920 | tf_op jit(solution)/shard_map/ppermute | solution.py:207
  4.0 90.9 %collective-permute-start.3 = (bf16[4096,512]{1,0:T(8,128)(2,1)}, bf16[4096,512]{1,0:T(8,128)(2,1)}, u32[]{:S(2)}, u32[]{:S(2)}) collective-permute-start(bf16[4096,512]{1,0:T(8,128)(2,1)} %refs_2_.5), channel_id=1, source_target_pairs={{0,1},{1,0},{2,3},{3,2},{4,5},{5,4},{6,7},{7,6}} | collective-permute-start | bytes 12582920 | tf_op jit(solution)/shard_map/ppermute | solution.py:207
  4.0 165.4 %collective-permute-start = (bf16[4096,512]{1,0:T(8,128)(2,1)}, bf16[4096,512]{1,0:T(8,128)(2,1)}, u32[]{:S(2)}, u32[]{:S(2)}) collective-permute-start(bf16[4096,512]{1,0:T(8,128)(2,1)} %refs_1_.13), channel_id=1, source_target_pairs={{0,2},{1,3},{2,0},{3,1},{4,6},{5,7},{6,4},{7,5}} | collective-permute-start | bytes 12582920 | tf_op jit(solution)/shard_map/ppermute | solution.py:207
  94.9 149.0 %collective-permute-start.2 = (bf16[4096,512]{1,0:T(8,128)(2,1)}, bf16[4096,512]{1,0:T(8,128)(2,1)}, u32[]{:S(2)}, u32[]{:S(2)}) collective-permute-start(bf16[4096,512]{1,0:T(8,128)(2,1)} %collective-permute-done.1.refs_2_), channel_id=1, source_target_pairs={{0,1},{1,0},{2,3},{3,2},{4,5},{5,4},{6,7},{7,6}} | collective-permute-start | bytes 12582920 | tf_op jit(solution)/shard_map/ppermute | solution.py:207
  392.4 117.0 %collective-permute-start.4 = (f32[4096,512]{1,0:T(8,128)}, f32[4096,512]{1,0:T(8,128)}, u32[]{:S(2)}, u32[]{:S(2)}) collective-permute-start(f32[4096,512]{1,0:T(8,128)} %get-tuple-element.57), channel_id=1, source_target_pairs={{0,1},{1,0},{2,3},{3,2},{4,5},{5,4},{6,7},{7,6}} | collective-permute-start | bytes 25165832 | tf_op jit(solution)/shard_map/ppermute | solution.py:207
  507.6 130.8 %collective-permute-start.5 = (f32[2048,512]{1,0:T(8,128)}, f32[2048,512]{1,0:T(8,128)}, u32[]{:S(2)}, u32[]{:S(2)}) collective-permute-start(f32[2048,512]{1,0:T(8,128)} %get-tuple-element.72), channel_id=1, source_target_pairs={{0,2},{1,3},{2,0},{3,1},{4,6},{5,7},{6,4},{7,5}} | collective-permute-start | bytes 12582920 | tf_op jit(solution)/shard_map/ppermute | solution.py:207
  590.0 260.1 %collective-permute-start.7 = (f32[4096,512]{1,0:T(8,128)}, f32[4096,512]{1,0:T(8,128)}, u32[]{:S(2)}, u32[]{:S(2)}) collective-permute-start(f32[4096,512]{1,0:T(8,128)} %get-tuple-element.75), channel_id=1, source_target_pairs={{0,1},{1,0},{2,3},{3,2},{4,5},{5,4},{6,7},{7,6}} | collective-permute-start | bytes 25165832 | tf_op jit(solution)/shard_map/ppermute | solution.py:207
  590.0 249.8 %collective-permute-start.6 = (f32[2048,512]{1,0:T(8,128)}, f32[2048,512]{1,0:T(8,128)}, u32[]{:S(2)}, u32[]{:S(2)}) collective-permute-start(f32[2048,512]{1,0:T(8,128)} %get-tuple-element.73), channel_id=1, source_target_pairs={{0,2},{1,3},{2,0},{3,1},{4,6},{5,7},{6,4},{7,5}} | collective-permute-start | bytes 12582920 | tf_op jit(solution)/shard_map/ppermute | solution.py:207
  636.4 213.7 %collective-permute-start.10 = (f32[1024,512]{1,0:T(8,128)}, f32[1024,512]{1,0:T(8,128)}, u32[]{:S(2)}, u32[]{:S(2)}) collective-permute-start(f32[1024,512]{1,0:T(8,128)} %get-tuple-element.78), channel_id=1, source_target_pairs={{0,4},{1,5},{2,6},{3,7},{4,0},{5,1},{6,2},{7,3}} | collective-permute-start | bytes 6291464 | tf_op jit(solution)/shard_map/ppermute | solution.py:207
  638.1 211.9 %collective-permute-start.9 = (f32[1024,512]{1,0:T(8,128)}, f32[1024,512]{1,0:T(8,128)}, u32[]{:S(2)}, u32[]{:S(2)}) collective-permute-start(f32[1024,512]{1,0:T(8,128)} %get-tuple-element.77), channel_id=1, source_target_pairs={{0,4},{1,5},{2,6},{3,7},{4,0},{5,1},{6,2},{7,3}} | collective-permute-start | bytes 6291464 | tf_op jit(solution)/shard_map/ppermute | solution.py:207
  638.4 211.6 %collective-permute-start.8 = (f32[2048,512]{1,0:T(8,128)}, f32[2048,512]{1,0:T(8,128)}, u32[]{:S(2)}, u32[]{:S(2)}) collective-permute-start(f32[2048,512]{1,0:T(8,128)} %get-tuple-element.76), channel_id=1, source_target_pairs={{0,4},{1,5},{2,6},{3,7},{4,0},{5,1},{6,2},{7,3}} | collective-permute-start | bytes 12582920 | tf_op jit(solution)/shard_map/ppermute | solution.py:207
  839.8 11.3 %copy-start = (f32[4096,512]{1,0:T(8,128)S(1)}, f32[4096,512]{1,0:T(8,128)}, u32[]{:S(2)}) copy-start(f32[4096,512]{1,0:T(8,128)} %get-tuple-element.74) | copy-start | bytes 25165828

commit v3 on v2

--- a/solution.py
+++ b/solution.py
@@ -234,12 +234,13 @@
         ig_x, tg_yp, st = block_call(sc, img_x, txt_yp, ig_x, None, st, **back)
         ig_own, tg_yp, st = block_call(sc, img_own, txt_yp, ig_own, tg_yp, st, **back)
         from_yp = swap(tg_yp, CORE)
-        tg_own, ig_x, st = block_call(sc, img_x, txt_own, tg_own, ig_x, st)
-        tg_p, ig_x0, st = block_call(sc, img_x, txt_p, tg_p, ig_x, st, irange=(0, half), keep_rows=cut)
+        tg_own, ig_x0, st = block_call(sc, img_x, txt_own, tg_own, ig_x, st, irange=(0, half), keep_rows=cut)
+        tg_p, ig_x0, st = block_call(sc, img_x, txt_p, tg_p, ig_x0, st, irange=(0, half), keep_rows=cut)
         from_x0 = swap(ig_x0, X)
         ig_own, tg_y0, st = block_call(sc, img_own, txt_y, ig_own, tg_y, st, jrange=(0, half), keep_rows=cut, extra=from_yp, **back)
         from_y0 = swap(tg_y0, Y)
-        tg_p, ig_x1, st = block_call(sc, img_x, txt_p, tg_p, ig_x, st, irange=(half, nb), keep_rows=cut, keep_off=half)
+        tg_own, ig_x1, st = block_call(sc, img_x, txt_own, tg_own, ig_x, st, irange=(half, nb), keep_rows=cut, keep_off=half)
+        tg_p, ig_x1, st = block_call(sc, img_x, txt_p, tg_p, ig_x1, st, irange=(half, nb), keep_rows=cut, keep_off=half)
         from_x1 = swap(ig_x1, X)
         from_p = swap(tg_p, CORE)
         last = cut - TILE
@@ -253,7 +254,10 @@
         img_grad = (ig_own + jnp.concatenate([from_x0, from_x1])) * factor
         txt_grad = (tg_own + from_p + jnp.concatenate([from_y0, from_y1, from_y2])) * factor
         sums = jnp.sum(st, axis=(1, 2))
-        sums = lax.psum(jnp.stack([sums[0] * LN2 + sums[1], sums[2], sums[3]]), axis_name)
+        sums = jnp.stack([sums[0] * LN2 + sums[1], sums[2], sums[3]])
+        sums = sums + swap(sums, CORE)
+        sums = sums + swap(sums, X)
+        sums = sums + swap(sums, Y)
         return (sums[0:1] / n_total, img_grad, txt_grad, sums[2:3] * factor, sums[1:2] / n_total)
 
     return jax.shard_map(per_device, mesh=mesh, in_specs=(P(axis_name, None), P(axis_name, None), P(None), P(None)), out_specs=(P(None), P(axis_name, None), P(axis_name, None), P(None), P(None)), check_vma=False)

time: 872 us -> 826 us (0.947)
  blocking collectives: 131 us -> 0 us
  waiting for transfers between devices: 64.1 us -> 145 us
    psum x1 -> x0, blocking collectives: 131 us -> none  [per_device(): lax.psum(jnp.stack([sums[0] * LN2 + sums[1], sums[2], sums[3]]), axis_name)]
    ppermute x11 -> x14, waiting for transfers between devices: 64.1 us -> 145 us  [swap(): return lax.ppermute(x, axis_name, [(d, d ^ bit) for d in range(n_dev)])]
    pallas_call x12 -> x13, Pallas kernels: 625 us -> 630 us  [block_call(): pl.pallas_call(kernel, grid=grid, in_specs=in_specs, out_specs=[nspec(n0)...]
  transfers between devices with their start and end apart: 11 -> 14, of which waited for: 1 -> 5; matrix products, arithmetic and copies ran while one was open for 2% -> 2% of each run, Pallas kernels for 55% -> 59%
where the time goes in v3:
time: 826 us; the launch traced here: 819 us
  Pallas kernels  630 us (76%)
  waiting for transfers between devices  145 us (18%)
  other arithmetic  19.8 us (2%)
  starting transfers between devices  13.4 us (2%)
  between operations  9.12 us (1%)
    pallas_call x13, Pallas kernels, block_call(): pl.pallas_call(kernel, grid=grid, in_specs=in_specs, out_specs=[nspec(n0)...  630 us
    ppermute x14, waiting for transfers between devices, swap(): return lax.ppermute(x, axis_name, [(d, d ^ bit) for d in range(n_dev)])  145 us
  transfers between devices with their start and end apart: 14, of which 5 were waited for; matrix products, arithmetic and copies ran while one was open for 2% of the time, Pallas kernels for 59%

profile of v3, /device:TPU:0, one launch (start us, length us, event | category | flops | bytes accessed | tf_op | source)
XLA Modules:
  0.0 819.4 jit_solution(9779345345604986755)
XLA Ops:
  0.6 3.4 collective-permute-start.1
  4.0 1.5 collective-permute-start
  6.8 0.6 pad_maximum_fusion.refs_0_
  7.4 0.6 broadcast_in_dim.3.refs_3_
  8.0 22.7 %pair_block.13 = (f32[4096,512]{1,0:T(8,128)}, f32[4096,512]{1,0:T(8,128)}, f32[4,8,128]{2,1,0:T(8,128)}, f32[4096,512]{1,0:T(8,128)}) custom-call(f32[4]{0:T(128)} %pad_maximum_fusion.refs_0_, bf16[4096,512]{1,0:T(8,128)(2,1)} %refs_1_.13, bf16[4096,512]{1,0:T(8,128)(2,1)} %refs_2_.7, ...), custom_call_target="tpu_custom_call", output_to_operand_aliasing={{2}: (3, {})} | custom-call | flops 12884901888 | bytes 41943040 | tf_op jit(solution)/shard_map/pair_block/pallas_call | solution.py:184
  30.8 64.1 %collective-permute-done.1.refs_2_ = bf16[4096,512]{1,0:T(8,128)(2,1)} collective-permute-done((bf16[4096,512]{1,0:T(8,128)(2,1)}, bf16[4096,512]{1,0:T(8,128)(2,1)}, u32[]{:S(2)}, u32[]{:S(2)}) %collective-permute-start.1) | collective-permute-done | bytes 4194336 | tf_op jit(solution)/shard_map/ppermute | solution.py:207
  94.9 74.5 %pair_block.14 = (f32[4096,512]{1,0:T(8,128)}, f32[4096,512]{1,0:T(8,128)}, f32[4,8,128]{2,1,0:T(8,128)}) custom-call(f32[4]{0:T(128)} %pad_maximum_fusion.refs_0_, bf16[4096,512]{1,0:T(8,128)(2,1)} %refs_1_.13, bf16[4096,512]{1,0:T(8,128)(2,1)} %collective-permute-done.3.refs_2_, ...), custom_call_target="tpu_custom_call", output_to_operand_aliasing={{0}: (3, {}), {2}: (4, {})} | custom-call | flops 51539607552 | bytes 41943040 | tf_op jit(solution)/shard_map/pair_block/pallas_call | solution.py:184
  169.4 74.4 %pair_block.15 = (f32[4096,512]{1,0:T(8,128)}, f32[4096,512]{1,0:T(8,128)}, f32[4,8,128]{2,1,0:T(8,128)}) custom-call(f32[4]{0:T(128)} %pad_maximum_fusion.refs_0_, bf16[4096,512]{1,0:T(8,128)(2,1)} %collective-permute-done.refs_1_, bf16[4096,512]{1,0:T(8,128)(2,1)} %collective-permute-done.1.refs_2_, ...), custom_call_target="tpu_custom_call", output_to_operand_aliasing={{0}: (3, {}), {2}: (4, {})} | custom-call | flops 51539607552 | bytes 41943040 | tf_op jit(solution)/shard_map/pair_block/pallas_call | solution.py:184
  243.9 74.0 %pair_block.16 = (f32[4096,512]{1,0:T(8,128)}, f32[4096,512]{1,0:T(8,128)}, f32[4,8,128]{2,1,0:T(8,128)}) custom-call(f32[4]{0:T(128)} %pad_maximum_fusion.refs_0_, bf16[4096,512]{1,0:T(8,128)(2,1)} %collective-permute-done.refs_1_, bf16[4096,512]{1,0:T(8,128)(2,1)} %collective-permute-done.2.refs_2_, ...), custom_call_target="tpu_custom_call", output_to_operand_aliasing={{0}: (3, {}), {2}: (4, {})} | custom-call | flops 51539607552 | bytes 41943040 | tf_op jit(solution)/shard_map/pair_block/pallas_call | solution.py:184
  317.8 74.5 %pair_block.17 = (f32[4096,512]{1,0:T(8,128)}, f32[4096,512]{1,0:T(8,128)}, f32[4,8,128]{2,1,0:T(8,128)}) custom-call(f32[4]{0:T(128)} %pad_maximum_fusion.refs_0_, bf16[4096,512]{1,0:T(8,128)(2,1)} %refs_1_.13, bf16[4096,512]{1,0:T(8,128)(2,1)} %collective-permute-done.2.refs_2_, ...), custom_call_target="tpu_custom_call", output_to_operand_aliasing={{0}: (3, {}), {1}: (4, {}), {2}: (5, {})} | custom-call | flops 51539607552 | bytes 41943040 | tf_op jit(solution)/shard_map/pair_block/pallas_call | solution.py:184
  392.3 0.5 collective-permute-start.4
  392.9 40.1 %pair_block.18 = (f32[4096,512]{1,0:T(8,128)}, f32[2048,512]{1,0:T(8,128)}, f32[4,8,128]{2,1,0:T(8,128)}) custom-call(f32[4]{0:T(128)} %pad_maximum_fusion.refs_0_, bf16[4096,512]{1,0:T(8,128)(2,1)} %collective-permute-done.refs_1_, bf16[4096,512]{1,0:T(8,128)(2,1)} %refs_2_.7, ...), custom_call_target="tpu_custom_call", output_to_operand_aliasing={{0}: (3, {}), {2}: (5, {})} | custom-call | flops 25769803776 | bytes 41943040 | tf_op jit(solution)/shard_map/pair_block/pallas_call | solution.py:184
  433.0 40.0 %pair_block.19 = (f32[4096,512]{1,0:T(8,128)}, f32[2048,512]{1,0:T(8,128)}, f32[4,8,128]{2,1,0:T(8,128)}) custom-call(f32[4]{0:T(128)} %pad_maximum_fusion.refs_0_, bf16[4096,512]{1,0:T(8,128)(2,1)} %collective-permute-done.refs_1_, bf16[4096,512]{1,0:T(8,128)(2,1)} %collective-permute-done.3.refs_2_, ...), custom_call_target="tpu_custom_call", output_to_operand_aliasing={{0}: (3, {}), {1}: (4, {}), {2}: (5, {})} | custom-call | flops 25769803776 | bytes 41943040 | tf_op jit(solution)/shard_map/pair_block/pallas_call | solution.py:184
  472.9 1.7 collective-permute-start.8
  474.6 40.7 %pair_block.20 = (f32[4096,512]{1,0:T(8,128)}, f32[2048,512]{1,0:T(8,128)}, f32[4,8,128]{2,1,0:T(8,128)}) custom-call(f32[4]{0:T(128)} %pad_maximum_fusion.refs_0_, bf16[4096,512]{1,0:T(8,128)(2,1)} %refs_1_.13, bf16[4096,512]{1,0:T(8,128)(2,1)} %collective-permute-done.1.refs_2_, ...), custom_call_target="tpu_custom_call", output_to_operand_aliasing={{0}: (3, {}), {2}: (6, {})} | custom-call | flops 25769803776 | bytes 41943040 | tf_op jit(solution)/shard_map/pair_block/pallas_call | solution.py:184
  515.4 39.7 %pair_block.21 = (f32[4096,512]{1,0:T(8,128)}, f32[2048,512]{1,0:T(8,128)}, f32[4,8,128]{2,1,0:T(8,128)}) custom-call(f32[4]{0:T(128)} %pad_maximum_fusion.refs_0_, bf16[4096,512]{1,0:T(8,128)(2,1)} %collective-permute-done.refs_1_, bf16[4096,512]{1,0:T(8,128)(2,1)} %refs_2_.7, ...), custom_call_target="tpu_custom_call", output_to_operand_aliasing={{0}: (3, {}), {2}: (5, {})} | custom-call | flops 25769803776 | bytes 41943040 | tf_op jit(solution)/shard_map/pair_block/pallas_call | solution.py:184
  555.1 40.0 %pair_block.22 = (f32[4096,512]{1,0:T(8,128)}, f32[2048,512]{1,0:T(8,128)}, f32[4,8,128]{2,1,0:T(8,128)}) custom-call(f32[4]{0:T(128)} %pad_maximum_fusion.refs_0_, bf16[4096,512]{1,0:T(8,128)(2,1)} %collective-permute-done.refs_1_, bf16[4096,512]{1,0:T(8,128)(2,1)} %collective-permute-done.3.refs_2_, ...), custom_call_target="tpu_custom_call", output_to_operand_aliasing={{0}: (3, {}), {1}: (4, {}), {2}: (5, {})} | custom-call | flops 25769803776 | bytes 41943040 | tf_op jit(solution)/shard_map/pair_block/pallas_call | solution.py:184
  595.4 1.7 collective-permute-start.11
  597.1 22.8 %pair_block.23 = (f32[4096,512]{1,0:T(8,128)}, f32[1024,512]{1,0:T(8,128)}, f32[4,8,128]{2,1,0:T(8,128)}) custom-call(f32[4]{0:T(128)} %pad_maximum_fusion.refs_0_, bf16[4096,512]{1,0:T(8,128)(2,1)} %refs_1_.13, bf16[4096,512]{1,0:T(8,128)(2,1)} %collective-permute-done.1.refs_2_, ...), custom_call_target="tpu_custom_call", output_to_operand_aliasing={{0}: (3, {}), {2}: (6, {})} | custom-call | flops 12884901888 | bytes 41943040 | tf_op jit(solution)/shard_map/pair_block/pallas_call | solution.py:184
  620.0 22.9 %pair_block.24 = (f32[4096,512]{1,0:T(8,128)}, f32[1024,512]{1,0:T(8,128)}, f32[4,8,128]{2,1,0:T(8,128)}) custom-call(f32[4]{0:T(128)} %pad_maximum_fusion.refs_0_, bf16[4096,512]{1,0:T(8,128)(2,1)} %refs_1_.13, bf16[4096,512]{1,0:T(8,128)(2,1)} %collective-permute-done.1.refs_2_, ...), custom_call_target="tpu_custom_call", output_to_operand_aliasing={{0}: (3, {}), {2}: (6, {})} | custom-call | flops 12884901888 | bytes 41943040 | tf_op jit(solution)/shard_map/pair_block/pallas_call | solution.py:184
  642.9 63.7 %pair_block.25 = (f32[4096,512]{1,0:T(8,128)}, f32[4096,512]{1,0:T(8,128)}, f32[4,8,128]{2,1,0:T(8,128)}) custom-call(f32[4]{0:T(128)} %pad_maximum_fusion.refs_0_, bf16[4096,512]{1,0:T(8,128)(2,1)} %refs_1_.13, bf16[4096,512]{1,0:T(8,128)(2,1)} %refs_2_.7, ...), custom_call_target="tpu_custom_call", output_to_operand_aliasing={{0}: (3, {}), {1}: (4, {}), {2}: (5, {})} | custom-call | flops 38654705664 | bytes 41943040 | tf_op jit(solution)/shard_map/pair_block/pallas_call | solution.py:184
  706.7 0.8 reduce_sum.9
  707.6 0.6 fusion.3
  710.0 0.8 collective-permute-done.5
  710.9 1.5 collective-permute-start.6
  712.4 2.1 collective-permute-done.6
  714.8 1.7 collective-permute-start.7
  716.5 45.0 %collective-permute-done.7 = f32[3]{0:T(128)S(1)} collective-permute-done((f32[3]{0:T(128)S(1)}, f32[3]{0:T(128)S(1)}, u32[]{:S(2)}, u32[]{:S(2)}) %collective-permute-start.7) | collective-permute-done | bytes 44 | tf_op jit(solution)/shard_map/ppermute | solution.py:207
  761.8 0.6 fusion.2
  764.4 10.2 %fusion = f32[4096,512]{1,0:T(8,128)} fusion(f32[4096,512]{1,0:T(8,128)} %get-tuple-element.77, f32[2048,512]{1,0:T(8,128)} %collective-permute-done.9, f32[2048,512]{1,0:T(8,128)} %collective-permute-done.8, f32[]{:T(128)} %bitcast), kind=kLoop, calls=%fused_computation.1 | loop fusion | flops 6291456 | bytes 25165828 | tf_op jit(solution)/shard_map/mul | solution.py:254
  774.6 32.9 %collective-permute-done.12 = f32[1024,512]{1,0:T(8,128)S(1)} collective-permute-done((f32[1024,512]{1,0:T(8,128)}, f32[1024,512]{1,0:T(8,128)S(1)}, u32[]{:S(2)}, u32[]{:S(2)}) %collective-permute-start.12) | collective-permute-done | bytes 2097184 | tf_op jit(solution)/shard_map/ppermute | solution.py:207
  807.5 8.0 fusion.1
  (23 shorter events, 1.7 us)
Async XLA Ops:
  0.6 94.2 %collective-permute-start.1 = (bf16[4096,512]{1,0:T(8,128)(2,1)}, bf16[4096,512]{1,0:T(8,128)(2,1)}, u32[]{:S(2)}, u32[]{:S(2)}) collective-permute-start(bf16[4096,512]{1,0:T(8,128)(2,1)} %refs_2_.7), channel_id=1, source_target_pairs={{0,4},{1,5},{2,6},{3,7},{4,0},{5,1},{6,2},{7,3}} | collective-permute-start | bytes 12582920 | tf_op jit(solution)/shard_map/ppermute | solution.py:207
  4.0 90.9 %collective-permute-start.3 = (bf16[4096,512]{1,0:T(8,128)(2,1)}, bf16[4096,512]{1,0:T(8,128)(2,1)}, u32[]{:S(2)}, u32[]{:S(2)}) collective-permute-start(bf16[4096,512]{1,0:T(8,128)(2,1)} %refs_2_.7), channel_id=1, source_target_pairs={{0,1},{1,0},{2,3},{3,2},{4,5},{5,4},{6,7},{7,6}} | collective-permute-start | bytes 12582920 | tf_op jit(solution)/shard_map/ppermute | solution.py:207
  4.0 165.4 %collective-permute-start = (bf16[4096,512]{1,0:T(8,128)(2,1)}, bf16[4096,512]{1,0:T(8,128)(2,1)}, u32[]{:S(2)}, u32[]{:S(2)}) collective-permute-start(bf16[4096,512]{1,0:T(8,128)(2,1)} %refs_1_.13), channel_id=1, source_target_pairs={{0,2},{1,3},{2,0},{3,1},{4,6},{5,7},{6,4},{7,5}} | collective-permute-start | bytes 12582920 | tf_op jit(solution)/shard_map/ppermute | solution.py:207
  94.9 149.0 %collective-permute-start.2 = (bf16[4096,512]{1,0:T(8,128)(2,1)}, bf16[4096,512]{1,0:T(8,128)(2,1)}, u32[]{:S(2)}, u32[]{:S(2)}) collective-permute-start(bf16[4096,512]{1,0:T(8,128)(2,1)} %collective-permute-done.1.refs_2_), channel_id=1, source_target_pairs={{0,1},{1,0},{2,3},{3,2},{4,5},{5,4},{6,7},{7,6}} | collective-permute-start | bytes 12582920 | tf_op jit(solution)/shard_map/ppermute | solution.py:207
  392.3 82.3 %collective-permute-start.4 = (f32[4096,512]{1,0:T(8,128)}, f32[4096,512]{1,0:T(8,128)}, u32[]{:S(2)}, u32[]{:S(2)}) collective-permute-start(f32[4096,512]{1,0:T(8,128)} %get-tuple-element.60), channel_id=1, source_target_pairs={{0,1},{1,0},{2,3},{3,2},{4,5},{5,4},{6,7},{7,6}} | collective-permute-start | bytes 25165832 | tf_op jit(solution)/shard_map/ppermute | solution.py:207
  472.9 241.8 %collective-permute-start.8 = (f32[2048,512]{1,0:T(8,128)}, f32[2048,512]{1,0:T(8,128)}, u32[]{:S(2)}, u32[]{:S(2)}) collective-permute-start(f32[2048,512]{1,0:T(8,128)} %get-tuple-element.78), channel_id=1, source_target_pairs={{0,2},{1,3},{2,0},{3,1},{4,6},{5,7},{6,4},{7,5}} | collective-permute-start | bytes 12582920 | tf_op jit(solution)/shard_map/ppermute | solution.py:207
  595.1 169.3 %collective-permute-start.9 = (f32[2048,512]{1,0:T(8,128)}, f32[2048,512]{1,0:T(8,128)}, u32[]{:S(2)}, u32[]{:S(2)}) collective-permute-start(f32[2048,512]{1,0:T(8,128)} %get-tuple-element.79), channel_id=1, source_target_pairs={{0,2},{1,3},{2,0},{3,1},{4,6},{5,7},{6,4},{7,5}} | collective-permute-start | bytes 12582920 | tf_op jit(solution)/shard_map/ppermute | solution.py:207
  595.4 212.1 %collective-permute-start.11 = (f32[2048,512]{1,0:T(8,128)}, f32[2048,512]{1,0:T(8,128)}, u32[]{:S(2)}, u32[]{:S(2)}) collective-permute-start(f32[2048,512]{1,0:T(8,128)} %get-tuple-element.82), channel_id=1, source_target_pairs={{0,4},{1,5},{2,6},{3,7},{4,0},{5,1},{6,2},{7,3}} | collective-permute-start | bytes 12582920 | tf_op jit(solution)/shard_map/ppermute | solution.py:207
  597.1 210.4 %collective-permute-start.10 = (f32[4096,512]{1,0:T(8,128)}, f32[4096,512]{1,0:T(8,128)}, u32[]{:S(2)}, u32[]{:S(2)}) collective-permute-start(f32[4096,512]{1,0:T(8,128)} %get-tuple-element.81), channel_id=1, source_target_pairs={{0,1},{1,0},{2,3},{3,2},{4,5},{5,4},{6,7},{7,6}} | collective-permute-start | bytes 25165832 | tf_op jit(solution)/shard_map/ppermute | solution.py:207
  709.5 1.3 collective-permute-start.5
  710.9 3.6 collective-permute-start.6
  714.5 60.1 %collective-permute-start.13 = (f32[1024,512]{1,0:T(8,128)}, f32[1024,512]{1,0:T(8,128)S(1)}, u32[]{:S(2)}, u32[]{:S(2)}) collective-permute-start(f32[1024,512]{1,0:T(8,128)} %get-tuple-element.84), channel_id=1, source_target_pairs={{0,4},{1,5},{2,6},{3,7},{4,0},{5,1},{6,2},{7,3}} | collective-permute-start | bytes 6291464 | tf_op jit(solution)/shard_map/ppermute | solution.py:207
  714.8 46.7 %collective-permute-start.7 = (f32[3]{0:T(128)S(1)}, f32[3]{0:T(128)S(1)}, u32[]{:S(2)}, u32[]{:S(2)}) collective-permute-start(f32[3]{0:T(128)S(1)} %add.29), channel_id=1, source_target_pairs={{0,4},{1,5},{2,6},{3,7},{4,0},{5,1},{6,2},{7,3}} | collective-permute-start | bytes 44 | tf_op jit(solution)/shard_map/ppermute | solution.py:207
  761.5 46.0 %collective-permute-start.12 = (f32[1024,512]{1,0:T(8,128)}, f32[1024,512]{1,0:T(8,128)S(1)}, u32[]{:S(2)}, u32[]{:S(2)}) collective-permute-start(f32[1024,512]{1,0:T(8,128)} %get-tuple-element.83), channel_id=1, source_target_pairs={{0,4},{1,5},{2,6},{3,7},{4,0},{5,1},{6,2},{7,3}} | collective-permute-start | bytes 6291464 | tf_op jit(solution)/shard_map/ppermute | solution.py:207
  764.4 43.2 %copy-start = (f32[4096,512]{1,0:T(8,128)S(1)}, f32[4096,512]{1,0:T(8,128)}, u32[]{:S(2)}) copy-start(f32[4096,512]{1,0:T(8,128)} %get-tuple-element.80) | copy-start | bytes 25165828
